TPU v7x, 32 devices: a whole 2x2x4 slice. The times are simulated.
32 devices in a mesh: gz: 4 (over y, core), tile: 8 (over z, x).
Axes of the slice: x: 2, y: 2, z: 4, core: 2. Of those that a mesh axis runs over, the one named last changes fastest.
Arguments:
- density: bfloat16 [32, 64, 512], P('gz', 'tile'), may hold values from -6 to 6
- w_first: bfloat16 [8, 1, 3, 3, 3], replicated, may hold values from -1.75 to 1.75
- b_first: float32 [8], replicated, may hold values from -1.25 to 1.25
- w_second: bfloat16 [8, 8, 3, 3, 3], replicated, may hold values from -0.5 to 0.5
- b_second: float32 [8], replicated, may hold values from -1.25 to 1.25
- w_third: bfloat16 [16, 8, 3, 3, 3], replicated, may hold values from -0.5 to 0.5
- b_third: float32 [16], replicated, may hold values from -1.25 to 1.25
- w_fourth: bfloat16 [16, 16, 3, 3, 3], replicated, may hold values from -0.4375 to 0.4375
- b_fourth: float32 [16], replicated, may hold values from -1.25 to 1.25
- w_fifth: bfloat16 [8, 24, 3, 3, 3], replicated, may hold values from -0.3125 to 0.3125
- b_fifth: float32 [8], replicated, may hold values from -1.25 to 1.25
- w_sixth: bfloat16 [8, 8, 3, 3, 3], replicated, may hold values from -0.5 to 0.5
- b_sixth: float32 [8], replicated, may hold values from -1.25 to 1.25
- w_head: bfloat16 [8], replicated, may hold values from -3 to 3
- b_head: float32 [1], replicated, may hold values from -1.75 to 1.75
Outputs:
- field: float32 [32, 64, 512], P('gz', 'tile')
All inputs are finite; a program needn't handle non-finite values.
Results may differ from a plain program's by a relative error of at most 0.012.
Values may be sent and summed in bfloat16 or wider, within the bound.
No kernel may reach another device: no remote copies, remote signals or barrier semaphores. Data moves between devices by JAX's collectives and lax.ppermute only.
A program may use at most 128 MiB of HBM per device.

v0:
```python
import numpy as np
import jax
import jax.numpy as jnp
from jax import lax
from jax.experimental import pallas as pl
from jax.experimental.pallas import tpu as pltpu
from jax.sharding import PartitionSpec as P

BF = jnp.bfloat16
F32 = jnp.float32
HALO = 8
GROUP = 8
GROUP5 = 6


def up(n, m):
    return -(-n // m) * m


def starts(total, size):
    size = min(size, total)
    s = list(range(0, total - size + 1, size))
    if s[-1] + size < total:
        s.append(total - size)
    return size, s


def lanes_of(dims, row_of, rows2_of, x_of, width):
    zs, xs, cs = dims
    t = np.full((3, width), -1, np.int32)
    for z in range(zs):
        for x in range(xs):
            for i in range(cs):
                c = (z * xs + x) * cs + i
                t[0, c] = row_of(z, x, i)
                t[1, c] = rows2_of(z, x, i)
                t[2, c] = x_of(z, x, i)
    return t


class Plan:
    def __init__(self, zl, xl, ny, cf, cc):
        h = HALO
        self.zl, self.xl, self.ny, self.cf, self.cc = zl, xl, ny, cf, cc
        self.nh = ny // 2
        self.zd, self.xd = zl + 2 * h, xl + 2 * h
        self.z1, self.x1 = self.zd - 2, self.xd - 2
        self.z2, self.x2 = self.zd - 4, self.xd - 4
        self.zp, self.xp = self.z2 // 2, self.x2 // 2
        self.z3, self.x3 = self.zp - 2, self.xp - 2
        self.z4, self.x4 = self.zp - 4, self.xp - 4
        self.zs, self.xs = zl + 4, xl + 4
        self.z5, self.x5 = zl + 2, xl + 2
        self.sx = up(3 * self.xd, 16)
        self.k1 = up(3 * self.sx, 128)
        self.g2, self.s2 = starts(self.x2, GROUP)
        self.g5, self.s5 = starts(self.x5, GROUP5)
        self.g6 = self.xl
        self.k2 = up(3 * (self.g2 + 2) * cf, 128)
        self.k3 = up(3 * self.xp * cf, 128)
        self.k4 = up(3 * self.x3 * cc, 128)
        self.k5 = up(3 * (self.g5 + 2) * cf, 128)
        self.kc = up(2 * self.x4 * cc, 128)
        self.k6 = up(3 * self.x5 * cf, 128)
        self.cells = zl * xl

    def tables(self):
        cf, cc = self.cf, self.cc
        n = 3 * cf + cc
        none = lambda z, x, i: -1
        xof = lambda z, x, i: x
        a2 = lanes_of((3, self.g2 + 2, cf), lambda z, x, i: z * n + i, none, xof, self.k2)
        a6 = lanes_of((3, self.x5, cf), lambda z, x, i: z * n + cf + i, none, xof, self.k6)
        a5 = lanes_of((3, self.g5 + 2, cf), lambda z, x, i: z * n + 2 * cf + i, none, xof, self.k5)
        o = 3 * cf
        ce = lanes_of(
            (2, self.x4, cc),
            lambda z, x, i: z * n + o + i,
            lambda z, x, i: 2 * n + o + i if z == 1 else -1,
            xof,
            self.kc,
        )
        co = lanes_of(
            (2, self.x4, cc),
            lambda z, x, i: 2 * z * n + o + i,
            lambda z, x, i: n + o + i if z == 0 else -1,
            xof,
            self.kc,
        )
        m = cf + cc
        b3 = lanes_of((3, self.xp, cf), lambda z, x, i: z * m + i, none, xof, self.k3)
        b4 = lanes_of((3, self.x3, cc), lambda z, x, i: z * m + cf + i, none, xof, self.k4)
        f1 = np.full((3, self.k1), -1, np.int32)
        for z in range(3):
            for dy in range(3):
                for x in range(self.xd):
                    c = z * self.sx + dy * self.xd + x
                    f1[0, c] = z * 3 + dy
                    f1[2, c] = x
        return [a2, a6, a5, ce, co, b3, b4, f1]


def prep_kernel(plan, widths, tab, wa, wb, w1, wh, a1, a2, a3, a4, a5, ac0, ac1, a6, hd, pm, pt):
    p = plan
    cf, cc = p.cf, p.cc
    off = np.concatenate([[0], np.cumsum(widths)]).tolist()

    def one_hot(i, j, rows):
        lo, hi = off[i], off[j]
        r = lax.broadcasted_iota(jnp.int32, (rows, hi - lo), 0)
        m = (r == tab[0:1, lo:hi]) | (r == tab[1:2, lo:hi])
        return jnp.where(m, 1.0, 0.0).astype(BF)

    def band(g, base, width, i, pick, outs, co, out_ref, dys):
        xi = tab[2:3, off[i] : off[i] + width]
        parts = []
        for dy in range(dys):
            for xo in range(outs):
                acc = jnp.zeros((co, width), F32)
                for dx in range(3):
                    r = (dx * dys + dy) * co
                    acc = acc + jnp.where(
                        xi == pick(xo, dx), g[r : r + co, base : base + width], 0.0
                    )
                parts.append(acc)
        out_ref[...] = jnp.concatenate(parts, axis=0).astype(BF)

    near = lambda xo, dx: xo + dx
    half = lambda xo, dx: (xo + dx) // 2
    ga = jnp.dot(wa[...], one_hot(0, 5, wa.shape[1]), preferred_element_type=F32)
    gb = jnp.dot(wb[...], one_hot(5, 7, wb.shape[1]), preferred_element_type=F32)
    g1 = jnp.dot(w1[...], one_hot(7, 8, w1.shape[1]), preferred_element_type=F32)
    band(g1, 0, p.k1, 7, near, p.x1, cf, a1, 1)
    band(ga, off[0], p.k2, 0, near, p.g2, cf, a2, 3)
    band(ga, off[1], p.k6, 1, near, p.xl, cf, a6, 3)
    band(ga, off[2], p.k5, 2, near, p.g5, cf, a5, 3)
    band(ga, off[3], p.kc, 3, half, p.x5, cf, ac0, 3)
    band(ga, off[4], p.kc, 4, half, p.x5, cf, ac1, 3)
    band(gb, 0, p.k3, 5, near, p.x3, cc, a3, 3)
    band(gb, p.k3, p.k4, 6, near, p.x4, cc, a4, 3)
    r = lax.broadcasted_iota(jnp.int32, (p.cells, p.cells * cf), 0)
    c = lax.broadcasted_iota(jnp.int32, (p.cells, p.cells * cf), 1)
    d = c - r * cf
    hd[...] = jnp.where((d >= 0) & (d < cf), wh[...], 0.0).astype(BF)
    r = lax.broadcasted_iota(jnp.int32, (p.ny, p.ny), 0)
    c = lax.broadcasted_iota(jnp.int32, (p.ny, p.ny), 1)
    fold = lambda k: jnp.where(k < p.nh, 2 * k, 2 * (k - p.nh) + 1)
    pm[...] = jnp.where(r == fold(c), 1.0, 0.0).astype(BF)
    pt[...] = jnp.where(c == fold(r), 1.0, 0.0).astype(BF)


def repeat(n, unroll, body):
    unroll = max(u for u in range(1, unroll + 1) if n % u == 0)
    if unroll == n:
        for k in range(n):
            body(k)
        return

    def step(t, carry):
        for k in range(unroll):
            body(t * unroll + k)
        return carry

    lax.fori_loop(0, n // unroll, step, 0)


def main_kernel(plan, *refs):
    p = plan
    blocks = refs[:9]
    (a1, a2, a3, a4, a5, ac0, ac1, a6, hd, pm, pt, bias, out) = refs[9:22]
    (dd, se, so, m1, sk, po, c1, c2, de, rf) = refs[22:]
    cf, cc, nh = p.cf, p.cc, p.nh
    b_first, b_second, b_third, b_fourth, b_fifth, b_sixth = (
        bias[lo:hi, :]
        for lo, hi in np.array(
            [
                (0, cf),
                (cf, 2 * cf),
                (2 * cf, 2 * cf + cc),
                (2 * cf + cc, 2 * cf + 2 * cc),
                (2 * cf + 2 * cc, 3 * cf + 2 * cc),
                (3 * cf + 2 * cc, 4 * cf + 2 * cc),
            ]
        ).tolist()
    )

    def dot(a, b):
        return jnp.dot(a, b, preferred_element_type=F32)

    def act(v, b, c):
        n = v.shape[0] // c
        u = v.reshape(n, c, nh) + b[None]
        return jnp.maximum(u, 0.1 * u).reshape(n * c, nh).astype(BF)

    def right(v):
        return pltpu.roll(v, 1, 1)

    def left(v):
        return pltpu.roll(v, nh - 1, 1)

    def window(ref, base, slab, rows, k, lo):
        parts = [
            ref[pl.ds(pl.multiple_of(base + dz * slab, 16), rows), lo : lo + nh] for dz in range(3)
        ]
        fill = k - 3 * rows
        while fill > 0:
            parts.append(parts[0][: min(fill, rows)])
            fill -= rows
        return jnp.concatenate(parts, axis=0)

    def taps(e, o, n):
        even = right(o[:n]) + e[n : 2 * n] + o[2 * n :]
        odd = e[:n] + o[n : 2 * n] + left(e[2 * n :])
        return even, odd

    h = HALO
    stacked = jnp.concatenate([b[...] for b in blocks], axis=0)
    split = dot(stacked, pm[...])
    row = 0
    for bz, nz in ((0, h), (h, p.zl), (h + p.zl, h)):
        for bx, nx in ((0, h), (h, p.xl), (h + p.xl, h)):
            dd[bz : bz + nz, bx : bx + nx, :] = split[row : row + nz * nx].reshape(nz, nx, p.ny)
            row += nz * nx

    def stack(z):
        e = dd[z, :, :nh]
        o = dd[z, :, nh:]
        pad = jnp.zeros((p.sx - 3 * p.xd, nh), F32)
        at = pl.ds(pl.multiple_of(z * p.sx, 16), p.sx)
        se[at, :] = jnp.concatenate([right(o), e, o, pad], axis=0).astype(BF)
        so[at, :] = jnp.concatenate([e, o, left(e), pad], axis=0).astype(BF)

    repeat(p.zd, 6, stack)
    tail = p.zd * p.sx
    se[tail:, :] = jnp.zeros((se.shape[0] - tail, nh), BF)
    so[tail:, :] = jnp.zeros((so.shape[0] - tail, nh), BF)

    r1 = p.x1 * cf

    def first(z):
        at = pl.ds(pl.multiple_of(z * p.sx, 16), p.k1)
        to = pl.ds(pl.multiple_of(z * r1, 16), r1)
        m1[to, :nh] = act(dot(a1[...], se[at, :]), b_first, cf)
        m1[to, nh:] = act(dot(a1[...], so[at, :]), b_first, cf)

    repeat(p.z1, 2, first)

    rp = p.xp * cf
    rs = p.xs * cf
    lead = (p.x2 - p.xs) // 2

    def second(zz):
        done = 0
        for s in p.s2:
            n = p.g2 * cf
            total = None
            skip = s + p.g2 - done
            new = (done - s) * cf
            for dz in range(2):
                base = (2 * zz + dz) * r1 + s * cf
                rows = (p.g2 + 2) * cf
                e = dot(a2[...], window(m1, base, r1, rows, p.k2, 0))
                o = dot(a2[...], window(m1, base, r1, rows, p.k2, nh))
                even, odd = taps(e, o, n)
                even = act(even[new:], b_second, cf)
                odd = act(odd[new:], b_second, cf)
                lo, hi = max(done, lead), min(s + p.g2, lead + p.xs)
                if lo < hi:
                    src = slice((lo - done) * cf, (hi - done) * cf)
                    to = pl.ds(
                        pl.multiple_of((2 * zz + dz) * rs + (lo - lead) * cf, 16), (hi - lo) * cf
                    )
                    sk[to, :nh] = even[src]
                    sk[to, nh:] = odd[src]
                t = even.astype(F32) + odd.astype(F32)
                t = t.reshape(skip // 2, 2, cf, nh)
                t = t[:, 0] + t[:, 1]
                total = t if total is None else total + t
            pooled = (0.125 * total).reshape(skip // 2 * cf, nh).astype(BF)
            po[pl.ds(pl.multiple_of(zz * rp + done // 2 * cf, 16), skip // 2 * cf), :] = pooled
            done = s + p.g2

    repeat(p.zp, 1, second)
    tail = p.zp * rp
    po[tail:, :] = jnp.zeros((po.shape[0] - tail, nh), BF)

    r3 = p.x3 * cc

    def third(z):
        v = dot(a3[...], po[pl.ds(pl.multiple_of(z * rp, 16), p.k3), :])
        v = right(v[:r3]) + v[r3 : 2 * r3] + left(v[2 * r3 :])
        c1[pl.ds(pl.multiple_of(z * r3, 16), r3), :] = act(v, b_third, cc)

    repeat(p.z3, 4, third)
    r4 = p.x4 * cc

    def fourth(z):
        v = dot(a4[...], window(c1, z * r3, r3, r3, p.k4, 0))
        v = right(v[:r4]) + v[r4 : 2 * r4] + left(v[2 * r4 :])
        c2[pl.ds(pl.multiple_of(z * r4, 16), r4), :] = act(v, b_fourth, cc)

    repeat(p.z4, 6, fourth)
    tail = p.z4 * r4
    c2[tail:, :] = jnp.zeros((c2.shape[0] - tail, nh), BF)
    r5 = p.x5 * cf
    skip_lead = (p.z2 - p.zs) // 2

    def fifth(pair):
        for odd_z in range(2):
            z = 2 * pair + odd_z
            ac = ac0 if odd_z else ac1
            q = dot(ac[...], c2[pl.ds(pl.multiple_of(pair * r4, 16), p.kc), :])
            q0, q1, q2 = q[:r5], q[r5 : 2 * r5], q[2 * r5 :]
            done = 0
            e3 = [[], [], []]
            o3 = [[], [], []]
            n = p.g5 * cf
            for s in p.s5:
                rows = (p.g5 + 2) * cf
                base = (z + skip_lead) * rs + s * cf
                e = dot(a5[...], window(sk, base, rs, rows, p.k5, 0))
                o = dot(a5[...], window(sk, base, rs, rows, p.k5, nh))
                new = (done - s) * cf
                for dy in range(3):
                    e3[dy].append(e[dy * n + new : (dy + 1) * n])
                    o3[dy].append(o[dy * n + new : (dy + 1) * n])
                done = s + p.g5
            e0, e1, e2 = (jnp.concatenate(v, axis=0) for v in e3)
            o0, o1, o2 = (jnp.concatenate(v, axis=0) for v in o3)
            even = right(o0 + q0) + (e1 + o2 + (q1 + q2))
            odd = (e0 + o1 + (q0 + q1)) + left(e2 + q2)
            to = pl.ds(pl.multiple_of(z * r5, 16), r5)
            de[to, :nh] = act(even, b_fifth, cf)
            de[to, nh:] = act(odd, b_fifth, cf)

    repeat(p.z5 // 2, 1, fifth)
    tail = p.z5 * r5
    de[tail:, :] = jnp.zeros((de.shape[0] - tail, p.ny), BF)
    r6 = p.xl * cf

    def sixth(z):
        at = pl.ds(pl.multiple_of(z * r5, 16), p.k6)
        e = dot(a6[...], de[at, :nh])
        o = dot(a6[...], de[at, nh:])
        even, odd = taps(e, o, r6)
        to = pl.ds(pl.multiple_of(z * r6, 16), r6)
        rf[to, :nh] = act(even, b_sixth, cf)
        rf[to, nh:] = act(odd, b_sixth, cf)

    repeat(p.zl, 4, sixth)
    last = 4 * cf + 2 * cc
    field = dot(hd[...], rf[...]) + bias[last : last + 1, 0:1]
    high = field.astype(BF)
    low = (field - high.astype(F32)).astype(BF)
    both = dot(jnp.concatenate([high, low], axis=0), pt[...])
    out[...] = both[: p.cells] + both[p.cells :]


def shift(block, axis, step):
    count = lax.axis_size(axis)
    return lax.ppermute(block, axis, [((i + step) % count, i) for i in range(count)])


def body(
    density,
    w_first,
    b_first,
    w_second,
    b_second,
    w_third,
    b_third,
    w_fourth,
    b_fourth,
    w_fifth,
    b_fifth,
    w_sixth,
    b_sixth,
    w_head,
    b_head,
):
    zl, xl, ny = density.shape
    cf, cc = w_second.shape[0], w_third.shape[0]
    h = HALO
    p = Plan(zl, xl, ny, cf, cc)

    left = shift(density[:, xl - h :], "tile", -1)
    right = shift(density[:, :h], "tile", 1)
    columns = [left, density, right]
    below = [shift(c[zl - h :], "gz", -1) for c in columns]
    above = [shift(c[:h], "gz", 1) for c in columns]
    blocks = [b.reshape(-1, ny) for b in below + columns + above]

    def table(w):
        return w.transpose(3, 4, 0, 2, 1).reshape(9 * w.shape[0], 3 * w.shape[1])

    wa = table(jnp.concatenate([w_second, w_sixth, w_fifth], axis=1))
    wb = table(jnp.concatenate([w_third, w_fourth], axis=1))
    w1 = w_first[:, 0].transpose(2, 0, 1, 3).reshape(3 * cf, 9)
    wh = jnp.tile(w_head.astype(F32), p.cells)[None]
    tabs = p.tables()
    widths = [t.shape[1] for t in tabs]
    tab = jnp.asarray(np.concatenate(tabs, axis=1))
    biases = jnp.concatenate(
        [b_first, b_second, b_third, b_fourth, b_fifth, b_sixth, jnp.tile(b_head, 8)]
    )
    bias = jnp.broadcast_to(biases[:, None], (biases.shape[0], p.nh))

    sds = jax.ShapeDtypeStruct
    mats = [
        sds((p.x1 * cf, p.k1), BF),
        sds((3 * p.g2 * cf, p.k2), BF),
        sds((3 * p.x3 * cc, p.k3), BF),
        sds((3 * p.x4 * cc, p.k4), BF),
        sds((3 * p.g5 * cf, p.k5), BF),
        sds((3 * p.x5 * cf, p.kc), BF),
        sds((3 * p.x5 * cf, p.kc), BF),
        sds((3 * p.xl * cf, p.k6), BF),
        sds((p.cells, p.cells * cf), BF),
        sds((ny, ny), BF),
        sds((ny, ny), BF),
    ]
    vmem = pl.BlockSpec(memory_space=pltpu.VMEM)
    tables = pl.pallas_call(
        lambda *refs: prep_kernel(p, widths, *refs),
        in_specs=[vmem] * 5,
        out_specs=[vmem] * len(mats),
        out_shape=mats,
        name="bands",
    )(tab, wa, wb, w1, wh)

    field = pl.pallas_call(
        lambda *refs: main_kernel(p, *refs),
        in_specs=[vmem] * (9 + len(mats) + 1),
        out_specs=vmem,
        out_shape=sds((p.cells, ny), F32),
        scratch_shapes=[
            pltpu.VMEM((p.zd, p.xd, ny), F32),
            pltpu.VMEM((p.zd * p.sx + 256, p.nh), BF),
            pltpu.VMEM((p.zd * p.sx + 256, p.nh), BF),
            pltpu.VMEM((p.z1 * p.x1 * cf, ny), BF),
            pltpu.VMEM((p.z2 * p.xs * cf, ny), BF),
            pltpu.VMEM((p.zp * p.xp * cf + 256, p.nh), BF),
            pltpu.VMEM((p.z3 * p.x3 * cc, p.nh), BF),
            pltpu.VMEM((p.z4 * p.x4 * cc + 256, p.nh), BF),
            pltpu.VMEM((p.z5 * p.x5 * cf + 256, ny), BF),
            pltpu.VMEM((p.cells * cf, ny), BF),
        ],
        name="unet",
    )(*blocks, *tables, bias)
    return field.reshape(zl, xl, ny)


def solution(mesh):
    return jax.shard_map(
        body,
        mesh=mesh,
        in_specs=(P("gz", "tile", None),) + (P(),) * 14,
        out_specs=P("gz", "tile", None),
        check_vma=False,
    )
```

profile of v0, /device:TPU:1, one launch (start us, length us, event | category | flops | bytes accessed | tf_op | source)
XLA Modules:
  0.0 38.2 jit_solution(13375554087161556777)
XLA Ops:
  0.0 5.1 %collective-permute-start.3 = (bf16[8,8,512]{2,1,0:T(8,128)(2,1)}, bf16[8,8,512]{2,1,0:T(8,128)(2,1)S(1)}, u32[]{:S(2)}, u32[]{:S(2)}) collective-permute-start(bf16[8,8,512]{2,1,0:T(8,128)(2,1)} %param.16), channel_id=1, source_target_pairs={{1,0},{2,1},{3,2},{4,3},{5,4},{6,5},{7,6},{0,7},{9,8},{10,9},{11,1... | collective-permute-start | bytes 196616 | tf_op jit(solution)/shard_map/ppermute | solution.py:361
  5.1 2.1 %collective-permute-start.2 = (bf16[8,8,512]{2,1,0:T(8,128)(2,1)}, bf16[8,8,512]{2,1,0:T(8,128)(2,1)S(1)}, u32[]{:S(2)}, u32[]{:S(2)}) collective-permute-start(bf16[8,8,512]{2,1,0:T(8,128)(2,1)} %param.16), channel_id=1, source_target_pairs={{24,0},{0,8},{8,16},{16,24},{25,1},{1,9},{9,17},{17,25},{26,2},{2,... | collective-permute-start | bytes 196616 | tf_op jit(solution)/shard_map/ppermute | solution.py:361
  7.1 0.0 collective-permute-start
  7.2 0.0 collective-permute-start.6
  7.8 0.7 %copy.24 = bf16[3,8,3,3]{1,0,3,2:T(4,128)(2,1)S(1)} copy(bf16[3,8,3,3]{1,3,0,2:T(4,128)(2,1)} %bitcast.30) | data formatting | bytes 864 | tf_op jit(solution)/shard_map/transpose | solution.py:398
  8.6 0.1 reshape.55
  8.7 0.7 %copy.25.refs_3_ = bf16[24,9]{1,0:T(8,128)(2,1)} copy(bf16[24,9]{0,1:T(8,128)(2,1)S(1)} %reshape.55) | data formatting | bytes 864 | tf_op jit(solution)/shard_map/reshape | solution.py:398
  9.4 0.7 %broadcast_in_dim_tile.3.refs_4_ = f32[1,512]{1,0:T(1,128)} reshape(f32[64,8]{1,0:T(8,128)S(1)} %tile.6) | data formatting | bytes 4096 | tf_op jit(solution)/shard_map/broadcast_in_dim;tile | solution.py:399
  10.0 0.9 %maximum_bitcast_fusion.1 = bf16[3,3,8,3,40]{4,2,1,0,3:T(8,128)(2,1)S(1)} fusion(bf16[8,24,3,3,3]{1,0,4,3,2:T(8,128)(2,1)S(1)} %copy-done.9, bf16[8,8,3,3,3]{1,0,4,3,2:T(8,128)(2,1)S(1)} %copy-done.10, bf16[8,8,3,3,3]{1,0,4,3,2:T(8,128)(2,1)} %param.19), kind=kLoop, calls=%fused_computation.1 | loop fusion | flops 51840 | bytes 34560 | tf_op jit(solution)/shard_map/transpose | solution.py:394
  11.0 0.0 copy-start.11
  11.0 0.0 copy-start
  11.0 0.7 %reshape.53.refs_1_ = bf16[72,120]{1,0:T(8,128)(2,1)} reshape(bf16[3,3,8,3,40]{4,3,2,1,0:T(4,128)(2,1)S(1)} %copy.21) | data formatting | bytes 34560 | tf_op jit(solution)/shard_map/reshape | solution.py:394
  11.7 0.1 copy-done.11
  11.8 0.1 copy.22
  11.9 0.7 %collective-permute-start.7 = (bf16[8,8,512]{2,1,0:T(8,128)(2,1)S(1)}, bf16[8,8,512]{2,1,0:T(8,128)(2,1)S(1)}, u32[]{:S(2)}, u32[]{:S(2)}) collective-permute-start(bf16[8,8,512]{2,1,0:T(8,128)(2,1)S(1)} %collective-permute-done.3), channel_id=1, source_target_pairs={{8,0},{16,8},{24,16},{0,24},{9,1},{17,9},{25,17},{1,25},{10,2},{18... | collective-permute-start | bytes 196616 | tf_op jit(solution)/shard_map/ppermute | solution.py:361
  12.6 1.2 %collective-permute-start.4 = (bf16[8,8,512]{2,1,0:T(8,128)(2,1)S(1)}, bf16[8,8,512]{2,1,0:T(8,128)(2,1)S(1)}, u32[]{:S(2)}, u32[]{:S(2)}) collective-permute-start(bf16[8,8,512]{2,1,0:T(8,128)(2,1)S(1)} %collective-permute-done.3), channel_id=1, source_target_pairs={{24,0},{0,8},{8,16},{16,24},{25,1},{1,9},{9,17},{17,25},{26,2},{2,... | collective-permute-start | bytes 196616 | tf_op jit(solution)/shard_map/ppermute | solution.py:361
  13.8 0.0 collective-permute-done
  13.8 0.0 collective-permute-start.5
  13.8 0.0 collective-permute-done.2
  13.8 1.7 %collective-permute-start.1 = (bf16[8,8,512]{2,1,0:T(8,128)(2,1)S(1)}, bf16[8,8,512]{2,1,0:T(8,128)(2,1)S(1)}, u32[]{:S(2)}, u32[]{:S(2)}) collective-permute-start(bf16[8,8,512]{2,1,0:T(8,128)(2,1)S(1)} %collective-permute-done), channel_id=1, source_target_pairs={{24,0},{0,8},{8,16},{16,24},{25,1},{1,9},{9,17},{17,25},{26,2},{2,... | collective-permute-start | bytes 196616 | tf_op jit(solution)/shard_map/ppermute | solution.py:361
  15.5 0.1 maximum_bitcast_fusion
  15.7 0.1 copy.23
  15.8 0.7 %reshape.54.refs_2_ = bf16[144,72]{1,0:T(8,128)(2,1)} reshape(bf16[3,3,16,3,24]{4,3,2,1,0:T(4,128)(2,1)S(1)} %copy.23) | data formatting | bytes 41472 | tf_op jit(solution)/shard_map/reshape | solution.py:394
  16.5 2.9 %bands.1 = (bf16[176,256]{1,0:T(8,128)(2,1)}, bf16[192,256]{1,0:T(8,128)(2,1)}, bf16[384,256]{1,0:T(8,128)(2,1)}, bf16[288,384]{1,0:T(8,128)(2,1)}, bf16[144,256...) custom-call(s32[3,2176]{1,0:T(4,128)} %constant.2.clone.refs_0_, ...), custom_call_target="tpu_custom_call" | custom-call | tf_op jit(solution)/shard_map/bands/pallas_call | solution.py:423
  19.4 0.0 copy-start.15
  19.4 0.6 %copy-done.13 = f32[8]{0:T(128)S(1)} copy-done((f32[8]{0:T(128)S(1)}, f32[8]{0:T(128)}, u32[]{:S(2)}) %copy-start.13) | copy-done | bytes 56
  20.0 0.0 copy-done.14
  20.0 0.0 copy-done.15
  20.0 0.1 concatenate.11
  20.1 0.0 collective-permute-done.7
  20.2 0.7 %broadcast_in_dim.2.refs_20_ = f32[72,256]{1,0:T(8,128)} broadcast(f32[72]{0:T(128)S(1)} %concatenate.11), dimensions={0} | broadcast | bytes 74016 | tf_op jit(solution)/shard_map/broadcast_in_dim | solution.py:406
  20.9 17.3 %unet.1 = f32[64,512]{1,0:T(8,128)} custom-call(bf16[64,512]{1,0:T(8,128)(2,1)} %bitcast.29, bf16[64,512]{1,0:T(8,128)(2,1)} %bitcast.23, bf16[64,512]{1,0:T(8,128)(2,1)} %bitcast.27, bf16[64,512]{1,0:T(8,128)(2,1)} %bitcast.24, bf16[64,512]{1,0:T(8,128)(2,1)} %bitcast.21, bf16[64,512]{1,0:T(8,128)(2,1)} %bitcast.22, bf16[64,512]{1,0:T(8,128)(2,1)} %bitcast.28, ...), custom_call_target="tpu_custom_call" | custom-call | tf_op jit(solution)/shard_map/unet/pallas_call | solution.py:431
  (39 shorter events, 0.1 us)
Async XLA Ops:
  0.0 11.9 %collective-permute-start.3 = (bf16[8,8,512]{2,1,0:T(8,128)(2,1)}, bf16[8,8,512]{2,1,0:T(8,128)(2,1)S(1)}, u32[]{:S(2)}, u32[]{:S(2)}) collective-permute-start(bf16[8,8,512]{2,1,0:T(8,128)(2,1)} %param.16), channel_id=1, source_target_pairs={{1,0},{2,1},{3,2},{4,3},{5,4},{6,5},{7,6},{0,7},{9,8},{10,9},{11,1... | collective-permute-start | bytes 196616 | tf_op jit(solution)/shard_map/ppermute | solution.py:361
  5.1 8.7 %collective-permute-start.2 = (bf16[8,8,512]{2,1,0:T(8,128)(2,1)}, bf16[8,8,512]{2,1,0:T(8,128)(2,1)S(1)}, u32[]{:S(2)}, u32[]{:S(2)}) collective-permute-start(bf16[8,8,512]{2,1,0:T(8,128)(2,1)} %param.16), channel_id=1, source_target_pairs={{24,0},{0,8},{8,16},{16,24},{25,1},{1,9},{9,17},{17,25},{26,2},{2,... | collective-permute-start | bytes 196616 | tf_op jit(solution)/shard_map/ppermute | solution.py:361
  7.1 6.6 %collective-permute-start = (bf16[8,8,512]{2,1,0:T(8,128)(2,1)}, bf16[8,8,512]{2,1,0:T(8,128)(2,1)S(1)}, u32[]{:S(2)}, u32[]{:S(2)}) collective-permute-start(bf16[8,8,512]{2,1,0:T(8,128)(2,1)} %param.16), channel_id=1, source_target_pairs={{7,0},{0,1},{1,2},{2,3},{3,4},{4,5},{5,6},{6,7},{15,8},{8,9},{9,10... | collective-permute-start | bytes 196616 | tf_op jit(solution)/shard_map/ppermute | solution.py:361
  7.2 13.0 %collective-permute-start.6 = (bf16[8,8,512]{2,1,0:T(8,128)(2,1)}, bf16[8,8,512]{2,1,0:T(8,128)(2,1)S(1)}, u32[]{:S(2)}, u32[]{:S(2)}) collective-permute-start(bf16[8,8,512]{2,1,0:T(8,128)(2,1)} %param.16), channel_id=1, source_target_pairs={{8,0},{16,8},{24,16},{0,24},{9,1},{17,9},{25,17},{1,25},{10,2},{18... | collective-permute-start | bytes 196616 | tf_op jit(solution)/shard_map/ppermute | solution.py:361
  7.2 2.2 %copy-start.12 = (bf16[8]{0:T(256)(128)(2,1)S(1)}, bf16[8]{0:T(256)(128)(2,1)}, u32[]{:S(2)}) copy-start(bf16[8]{0:T(256)(128)(2,1)} %param.29) | copy-start | bytes 52
  7.8 2.2 %copy-start.10 = (bf16[8,8,3,3,3]{1,0,4,3,2:T(8,128)(2,1)S(1)}, bf16[8,8,3,3,3]{1,0,4,3,2:T(8,128)(2,1)}, u32[]{:S(2)}) copy-start(bf16[8,8,3,3,3]{1,0,4,3,2:T(8,128)(2,1)} %param.27) | copy-start | bytes 10372
  7.8 2.2 %copy-start.9 = (bf16[8,24,3,3,3]{1,0,4,3,2:T(8,128)(2,1)S(1)}, bf16[8,24,3,3,3]{1,0,4,3,2:T(8,128)(2,1)}, u32[]{:S(2)}) copy-start(bf16[8,24,3,3,3]{1,0,4,3,2:T(8,128)(2,1)} %param.25) | copy-start | bytes 31108
  11.0 0.8 %copy-start.11 = (bf16[16,8,3,3,3]{0,1,4,3,2:T(8,128)(2,1)S(1)}, bf16[16,8,3,3,3]{0,1,4,3,2:T(8,128)(2,1)}, u32[]{:S(2)}) copy-start(bf16[16,8,3,3,3]{0,1,4,3,2:T(8,128)(2,1)} %param.21) | copy-start | bytes 20740
  11.0 4.5 %copy-start = (bf16[16,16,3,3,3]{1,0,4,3,2:T(8,128)(2,1)S(1)}, bf16[16,16,3,3,3]{1,0,4,3,2:T(8,128)(2,1)}, u32[]{:S(2)}) copy-start(bf16[16,16,3,3,3]{1,0,4,3,2:T(8,128)(2,1)} %param.23) | copy-start | bytes 41476
  11.9 3.7 %copy-start.1 = (bf16[8,8,512]{2,1,0:T(8,128)(2,1)}, bf16[8,8,512]{2,1,0:T(8,128)(2,1)S(1)}, u32[]{:S(2)}) copy-start(bf16[8,8,512]{2,1,0:T(8,128)(2,1)S(1)} %collective-permute-done.3) | copy-start | bytes 196612
  11.9 8.2 %collective-permute-start.7 = (bf16[8,8,512]{2,1,0:T(8,128)(2,1)S(1)}, bf16[8,8,512]{2,1,0:T(8,128)(2,1)S(1)}, u32[]{:S(2)}, u32[]{:S(2)}) collective-permute-start(bf16[8,8,512]{2,1,0:T(8,128)(2,1)S(1)} %collective-permute-done.3), channel_id=1, source_target_pairs={{8,0},{16,8},{24,16},{0,24},{9,1},{17,9},{25,17},{1,25},{10,2},{18... | collective-permute-start | bytes 196616 | tf_op jit(solution)/shard_map/ppermute | solution.py:361
  12.6 7.6 %collective-permute-start.4 = (bf16[8,8,512]{2,1,0:T(8,128)(2,1)S(1)}, bf16[8,8,512]{2,1,0:T(8,128)(2,1)S(1)}, u32[]{:S(2)}, u32[]{:S(2)}) collective-permute-start(bf16[8,8,512]{2,1,0:T(8,128)(2,1)S(1)} %collective-permute-done.3), channel_id=1, source_target_pairs={{24,0},{0,8},{8,16},{16,24},{25,1},{1,9},{9,17},{17,25},{26,2},{2,... | collective-permute-start | bytes 196616 | tf_op jit(solution)/shard_map/ppermute | solution.py:361
  13.8 1.9 %copy-start.3 = (bf16[8,8,512]{2,1,0:T(8,128)(2,1)}, bf16[8,8,512]{2,1,0:T(8,128)(2,1)S(1)}, u32[]{:S(2)}) copy-start(bf16[8,8,512]{2,1,0:T(8,128)(2,1)S(1)} %collective-permute-done) | copy-start | bytes 196612
  13.8 6.4 %collective-permute-start.5 = (bf16[8,8,512]{2,1,0:T(8,128)(2,1)S(1)}, bf16[8,8,512]{2,1,0:T(8,128)(2,1)S(1)}, u32[]{:S(2)}, u32[]{:S(2)}) collective-permute-start(bf16[8,8,512]{2,1,0:T(8,128)(2,1)S(1)} %collective-permute-done), channel_id=1, source_target_pairs={{8,0},{16,8},{24,16},{0,24},{9,1},{17,9},{25,17},{1,25},{10,2},{18... | collective-permute-start | bytes 196616 | tf_op jit(solution)/shard_map/ppermute | solution.py:361
  13.8 1.9 %copy-start.2 = (bf16[8,8,512]{2,1,0:T(8,128)(2,1)}, bf16[8,8,512]{2,1,0:T(8,128)(2,1)S(1)}, u32[]{:S(2)}) copy-start(bf16[8,8,512]{2,1,0:T(8,128)(2,1)S(1)} %collective-permute-done.2) | copy-start | bytes 196612
  13.8 6.4 %collective-permute-start.1 = (bf16[8,8,512]{2,1,0:T(8,128)(2,1)S(1)}, bf16[8,8,512]{2,1,0:T(8,128)(2,1)S(1)}, u32[]{:S(2)}, u32[]{:S(2)}) collective-permute-start(bf16[8,8,512]{2,1,0:T(8,128)(2,1)S(1)} %collective-permute-done), channel_id=1, source_target_pairs={{24,0},{0,8},{8,16},{16,24},{25,1},{1,9},{9,17},{17,25},{26,2},{2,... | collective-permute-start | bytes 196616 | tf_op jit(solution)/shard_map/ppermute | solution.py:361
  16.5 2.9 %copy-start.16 = (f32[16]{0:T(128)S(1)}, f32[16]{0:T(128)}, u32[]{:S(2)}) copy-start(f32[16]{0:T(128)} %param.24) | copy-start | bytes 196
  16.5 2.9 %copy-start.17 = (f32[8]{0:T(128)S(1)}, f32[8]{0:T(128)}, u32[]{:S(2)}) copy-start(f32[8]{0:T(128)} %param.26) | copy-start | bytes 100
  16.5 2.9 %copy-start.18 = (f32[8]{0:T(128)S(1)}, f32[8]{0:T(128)}, u32[]{:S(2)}) copy-start(f32[8]{0:T(128)} %param.28) | copy-start | bytes 100
  19.4 0.7 %copy-start.13 = (f32[8]{0:T(128)S(1)}, f32[8]{0:T(128)}, u32[]{:S(2)}) copy-start(f32[8]{0:T(128)} %param.18) | copy-start | bytes 100
  19.4 0.7 %copy-start.14 = (f32[8]{0:T(128)S(1)}, f32[8]{0:T(128)}, u32[]{:S(2)}) copy-start(f32[8]{0:T(128)} %param.20) | copy-start | bytes 100
  19.4 0.7 %copy-start.15 = (f32[16]{0:T(128)S(1)}, f32[16]{0:T(128)}, u32[]{:S(2)}) copy-start(f32[16]{0:T(128)} %param.22) | copy-start | bytes 196
  20.1 0.8 %copy-start.4 = (bf16[8,8,512]{2,1,0:T(8,128)(2,1)}, bf16[8,8,512]{2,1,0:T(8,128)(2,1)S(1)}, u32[]{:S(2)}) copy-start(bf16[8,8,512]{2,1,0:T(8,128)(2,1)S(1)} %collective-permute-done.6) | copy-start | bytes 196612
  20.1 0.8 %copy-start.5 = (bf16[8,8,512]{2,1,0:T(8,128)(2,1)}, bf16[8,8,512]{2,1,0:T(8,128)(2,1)S(1)}, u32[]{:S(2)}) copy-start(bf16[8,8,512]{2,1,0:T(8,128)(2,1)S(1)} %collective-permute-done.7) | copy-start | bytes 196612
  20.2 0.8 %copy-start.6 = (bf16[8,8,512]{2,1,0:T(8,128)(2,1)}, bf16[8,8,512]{2,1,0:T(8,128)(2,1)S(1)}, u32[]{:S(2)}) copy-start(bf16[8,8,512]{2,1,0:T(8,128)(2,1)S(1)} %collective-permute-done.4) | copy-start | bytes 196612
  20.2 0.7 %copy-start.7 = (bf16[8,8,512]{2,1,0:T(8,128)(2,1)}, bf16[8,8,512]{2,1,0:T(8,128)(2,1)S(1)}, u32[]{:S(2)}) copy-start(bf16[8,8,512]{2,1,0:T(8,128)(2,1)S(1)} %collective-permute-done.5) | copy-start | bytes 196612
  20.2 0.7 %copy-start.8 = (bf16[8,8,512]{2,1,0:T(8,128)(2,1)}, bf16[8,8,512]{2,1,0:T(8,128)(2,1)S(1)}, u32[]{:S(2)}) copy-start(bf16[8,8,512]{2,1,0:T(8,128)(2,1)S(1)} %collective-permute-done.1) | copy-start | bytes 196612
where the time goes:
time: 38.6 us; the launch traced here: 38.2 us
  Pallas kernels  20.1 us (52%)
  starting transfers between devices  10.7 us (28%)
  local copies, waits for them, and re-layouts  5.38 us (14%)
  other arithmetic  1.02 us (3%)
  between operations  0.92 us (2%)
    pallas_call x1, Pallas kernels, body(): pl.pallas_call(lambda *refs: main_kernel(p, *refs), in_specs=[vmem] * (9...  17.3 us
    ppermute x8, starting transfers between devices, shift(): lax.ppermute(block, axis, [((i + step) % count, i) for i in range(count)])  10.7 us
    pallas_call x1, Pallas kernels, body(): pl.pallas_call(lambda *refs: prep_kernel(p, widths, *refs), in_specs=[vme...  2.85 us
    reshape x2, local copies, waits for them, and re-layouts, table(): return w.transpose(3, 4, 0, 2, 1).reshape(9 * w.shape[0], 3 * w.shape[1])  1.44 us
    transpose x2, other arithmetic, table(): return w.transpose(3, 4, 0, 2, 1).reshape(9 * w.shape[0], 3 * w.shape[1])  1.02 us
    unnamed x39, local copies, waits for them, and re-layouts  0.87 us
    reshape x2, local copies, waits for them, and re-layouts, body(): w1 = w_first[:, 0].transpose(2, 0, 1, 3).reshape(3 * cf, 9)  0.78 us
  transfers between devices with their start and end apart: 8, of which 0 were waited for; matrix products, arithmetic and copies ran while one was open for 13% of the time, Pallas kernels for 7%

commit v1 on v0

v1 whole, which is shorter than its diff:
```python
import numpy as np
import jax
import jax.numpy as jnp
from jax import lax
from jax.experimental import pallas as pl
from jax.experimental.pallas import tpu as pltpu
from jax.sharding import PartitionSpec as P


BF = jnp.bfloat16
F32 = jnp.float32
HALO = 8
GROUP = 8
GROUP5 = 6
LANES = 128
U_STACK, U_FIRST, U_SECOND, U_THIRD, U_FOURTH, U_FIFTH, U_SIXTH = 6, 11, 2, 8, 6, 5, 8
MATS = 13
ORDER = (10, 12, 0, 1, 2, 3, 4, 5, 6, 7, 8, 9, 11)
CODE = 64


def up(n, m):
    return -(-n // m) * m


def starts(total, size):
    size = min(size, total)
    s = list(range(0, total - size + 1, size))
    if s[-1] + size < total:
        s.append(total - size)
    return size, s


def lanes_of(dims, row_of, rows2_of, x_of, width):
    zs, xs, cs = dims
    t = np.full((3, width), -1, np.int32)
    for z in range(zs):
        for x in range(xs):
            for i in range(cs):
                c = (z * xs + x) * cs + i
                t[0, c] = row_of(z, x, i)
                t[1, c] = rows2_of(z, x, i)
                t[2, c] = x_of(z, x, i)
    return t


class Plan:
    def __init__(self, zl, xl, ny, cf, cc):
        h = HALO
        self.zl, self.xl, self.ny, self.cf, self.cc = zl, xl, ny, cf, cc
        self.nh = ny // 2
        self.zd, self.xd = zl + 2 * h, xl + 2 * h
        self.z1, self.x1 = self.zd - 2, self.xd - 2
        self.z2, self.x2 = self.zd - 4, self.xd - 4
        self.zp, self.xp = self.z2 // 2, self.x2 // 2
        self.z3, self.x3 = self.zp - 2, self.xp - 2
        self.z4, self.x4 = self.zp - 4, self.xp - 4
        self.zs, self.xs = zl + 4, xl + 4
        self.z5, self.x5 = zl + 2, xl + 2
        self.sx = up(3 * self.xd, 16)
        self.k1 = up(3 * self.sx, 128)
        self.n2 = self.x2 // GROUP
        self.rest = self.x2 - self.n2 * GROUP
        self.g5, self.s5 = starts(self.x5, GROUP5)
        self.k2 = up(3 * (GROUP + 2) * cf, 128)
        self.kr = up(4 * (self.rest + 2) * cf, 128)
        self.k3 = up(3 * self.xp * cf, 128)
        self.k4 = up(3 * self.x3 * cc, 128)
        self.k5 = up(3 * (self.g5 + 2) * cf, 128)
        self.kc = up(2 * self.x4 * cc, 128)
        self.k6 = up(3 * self.x5 * cf, 128)
        self.cells = zl * xl
        self.span = 2 * LANES

    def tables(self):
        cf, cc = self.cf, self.cc
        none = lambda z, x, i: -1
        xof = lambda z, x, i: x
        code = lambda z, x, i: CODE * z + i
        a2 = lanes_of((3, GROUP + 2, cf), code, none, xof, self.k2)
        r0 = lanes_of((4, self.rest + 2, cf), lambda z, x, i: CODE * z + i if z < 3 else -1, none, xof, self.kr)
        r1 = lanes_of((4, self.rest + 2, cf), lambda z, x, i: CODE * (z - 1) + i if z else -1, none, xof, self.kr)
        a6 = lanes_of((3, self.x5, cf), code, none, xof, self.k6)
        a5 = lanes_of((3, self.g5 + 2, cf), code, none, xof, self.k5)
        ce = lanes_of(
            (2, self.x4, cc),
            lambda z, x, i: CODE * z + cf + i,
            lambda z, x, i: CODE * 2 + cf + i if z == 1 else -1,
            xof,
            self.kc,
        )
        co = lanes_of(
            (2, self.x4, cc),
            lambda z, x, i: CODE * 2 * z + cf + i,
            lambda z, x, i: CODE + cf + i if z == 0 else -1,
            xof,
            self.kc,
        )
        b4 = lanes_of((3, self.x3, cc), code, none, xof, self.k4)
        b3 = lanes_of((3, self.xp, cf), lambda z, x, i: 9 * cf * z + i, none, xof, self.k3)
        f1 = np.full((3, self.k1), -1, np.int32)
        for z in range(3):
            for dy in range(3):
                for x in range(self.xd):
                    c = z * self.sx + dy * self.xd + x
                    f1[0, c] = z * 24 + dy
                    f1[2, c] = x
        hd = lanes_of((1, self.cells, cf), lambda z, x, i: i, none, xof, self.cells * cf)
        return [a2, r0, r1, a6, a5, ce, co, b4, b3, f1, hd]


def prep_kernel(plan, widths, *refs):
    (tab, w2, w6, w5, w4, w3, w1, wh) = refs[:8]
    biases = refs[8:15]
    (a1, a2, ar, a3, a4, a5, ac0, ac1, a6, hd, pm, pt, bias) = refs[15:28]
    (t1,) = refs[28:]
    p = plan
    cf, cc = p.cf, p.cc
    off = np.concatenate([[0], np.cumsum(widths)]).tolist()

    def dot(a, b):
        return jnp.dot(a, b, preferred_element_type=F32)

    def expand(w, i, j, co):
        lo, hi = off[i], off[j]
        rows = w.shape[1]
        r = lax.broadcasted_iota(jnp.int32, (rows, hi - lo), 0)
        total = None
        for dz in range(3):
            m = (r + CODE * dz == tab[0:1, lo:hi]) | (r + CODE * dz == tab[1:2, lo:hi])
            g = dot(w[dz * 9 * co : (dz + 1) * 9 * co, :], jnp.where(m, 1.0, 0.0).astype(BF))
            total = g if total is None else total + g
        return total

    def select(w, i, base):
        lo, hi = off[i], off[i + 1]
        r = lax.broadcasted_iota(jnp.int32, (w.shape[1], hi - lo), 0)
        m = (r - base == tab[0:1, lo:hi]) & (tab[0:1, lo:hi] >= 0)
        return dot(w, jnp.where(m, 1.0, 0.0).astype(BF))

    def band(pieces, i, pick, outs):
        xi = tab[2:3, off[i] : off[i + 1]]
        parts = []
        for xo in range(outs):
            acc = None
            for dx in range(3):
                v = jnp.where(xi == pick(xo, dx), pieces[dx], 0.0)
                acc = v if acc is None else acc + v
            parts.append(acc)
        return parts

    def rows_of(g, lo, width, dy, co):
        return [
            g[(dx * 3 + dy) * co : (dx * 3 + dy + 1) * co, lo : lo + width] for dx in range(3)
        ]

    def full(out, g, lo, i, pick, outs, co):
        parts = []
        for dy in range(3):
            parts += band(rows_of(g, lo, widths[i], dy, co), i, pick, outs)
        out[...] = jnp.concatenate(parts, axis=0).astype(BF)

    near = lambda xo, dx: xo + dx
    half = lambda xo, dx: (xo + dx) // 2
    t1[...] = jnp.zeros(t1.shape, F32)
    for k in range(9):
        t1[8 * k : 8 * k + 3, :cf] = w1[k // 3, k % 3].astype(F32)
    turned = t1[...].T[:cf].astype(BF)
    a1[...] = jnp.concatenate(
        band([select(turned, 9, 8 * dx) for dx in range(3)], 9, near, p.x1), axis=0
    ).astype(BF)
    g = expand(w2, 0, 3, cf)
    full(a2, g, 0, 0, near, GROUP, cf)
    parts = []
    for dy in range(3):
        for zo in range(2):
            lo = off[1 + zo]
            parts += band(rows_of(g, lo, p.kr, dy, cf), 1 + zo, near, p.rest)
    if parts:
        ar[...] = jnp.concatenate(parts, axis=0).astype(BF)
    full(a6, expand(w6, 3, 4, cf), 0, 3, near, p.xl, cf)
    g = expand(w5, 4, 7, cf)
    full(a5, g, 0, 4, near, p.g5, cf)
    full(ac0, g, off[5] - off[4], 5, half, p.x5, cf)
    full(ac1, g, off[6] - off[4], 6, half, p.x5, cf)
    full(a4, expand(w4, 7, 8, cc), 0, 7, near, p.x4, cc)
    turned = w3[...].astype(F32).T.astype(BF)
    parts = []
    for dy in range(3):
        pieces = [select(turned, 8, (3 * dx + dy) * cf) for dx in range(3)]
        parts += band(pieces, 8, near, p.x3)
    a3[...] = jnp.concatenate(parts, axis=0).astype(BF)
    v = select(jnp.broadcast_to(wh[...], (16, cf)), 10, 0)
    r = lax.broadcasted_iota(jnp.int32, (p.cells, p.cells * cf), 0)
    cell = tab[2:3, off[10] : off[11]]
    hd[...] = jnp.where(cell == r, v[0:1], 0.0).astype(BF)
    r = lax.broadcasted_iota(jnp.int32, (p.span, p.span), 0)
    c = lax.broadcasted_iota(jnp.int32, (p.span, p.span), 1)
    fold = lambda k: jnp.where(k < LANES, 2 * k, 2 * (k - LANES) + 1)
    pm[...] = jnp.where(r == fold(c), 1.0, 0.0).astype(BF)
    pt[...] = jnp.where(c == fold(r), 1.0, 0.0).astype(BF)
    at = 0
    for b in biases:
        n = b.shape[0]
        m = up(n, 8)
        r = lax.broadcasted_iota(jnp.int32, (m, p.nh), 0)
        v = jnp.zeros((m, p.nh), F32)
        for k in range(n):
            v = jnp.where(r == k, b[k], v)
        bias[at : at + m, :] = v
        at += m


def repeat(n, unroll, body):
    unroll = max(u for u in range(1, unroll + 1) if n % u == 0)
    if unroll == n:
        for k in range(n):
            body(k)
        return

    def step(t, carry):
        for k in range(unroll):
            body(t * unroll + k)
        return carry

    lax.fori_loop(0, n // unroll, step, 0)


def main_kernel(plan, *refs):
    p = plan
    n = 9 + MATS
    out = refs[n]
    (dd, se, so, m1, sk, po, c1, c2, de, rf, raw) = refs[n + 1 : n + 12]
    mats = refs[n + 12 : n + 12 + MATS]
    sem = refs[n + 12 + MATS]
    (a1, a2, ar, a3, a4, a5, ac0, ac1, a6, hd, pm, pt, bias) = mats
    copies = []
    row = 0
    for k in range(9):
        rows = refs[k].shape[0]
        copies.append(pltpu.make_async_copy(refs[k], raw.at[pl.ds(row, rows)], sem.at[k]))
        row += rows
    for k in range(MATS):
        copies.append(pltpu.make_async_copy(refs[9 + k], mats[k], sem.at[9 + k]))
    for k in list(range(9)) + [9 + ORDER[k] for k in range(MATS)]:
        copies[k].start()

    def ready(*names):
        for k in names:
            copies[k].wait()

    cf, cc, nh = p.cf, p.cc, p.nh

    def rows(lo, n):
        return bias[lo : lo + n, :]

    def dot(a, b):
        return jnp.dot(a, b, preferred_element_type=F32)

    def act(v, b, c):
        n = v.shape[0] // c
        u = v.reshape(n, c, nh) + b[None]
        return jnp.maximum(u, 0.1 * u).reshape(n * c, nh).astype(BF)

    def right(v):
        return pltpu.roll(v, 1, 1)

    def left(v):
        return pltpu.roll(v, nh - 1, 1)

    def window(ref, base, slab, rows, k, lo, slabs=3):
        parts = [
            ref[pl.ds(pl.multiple_of(base + dz * slab, 16), rows), lo : lo + nh]
            for dz in range(slabs)
        ]
        fill = k - slabs * rows
        while fill > 0:
            parts.append(parts[0][: min(fill, rows)])
            fill -= rows
        return jnp.concatenate(parts, axis=0)

    def taps(e, o, n):
        even = right(o[:n]) + e[n : 2 * n] + o[2 * n :]
        odd = e[:n] + o[n : 2 * n] + left(e[2 * n :])
        return even, odd

    h = HALO
    ready(*range(9), 9 + 10)
    span = p.span
    split = [dot(raw[:, y : y + span], pm[...]) for y in range(0, p.ny, span)]
    row = 0
    for bz, nz in ((0, h), (h, p.zl), (h + p.zl, h)):
        for bx, nx in ((0, h), (h, p.xl), (h + p.xl, h)):
            for k, v in enumerate(split):
                v = v[row : row + nz * nx].reshape(nz, nx, span)
                at = slice(k * LANES, (k + 1) * LANES)
                dd[bz : bz + nz, bx : bx + nx, at] = v[:, :, :LANES]
                at = slice(nh + k * LANES, nh + (k + 1) * LANES)
                dd[bz : bz + nz, bx : bx + nx, at] = v[:, :, LANES:]
            row += nz * nx

    def stack(z):
        e = dd[z, :, :nh]
        o = dd[z, :, nh:]
        pad = jnp.zeros((p.sx - 3 * p.xd, nh), F32)
        at = pl.ds(pl.multiple_of(z * p.sx, 16), p.sx)
        se[at, :] = jnp.concatenate([right(o), e, o, pad], axis=0).astype(BF)
        so[at, :] = jnp.concatenate([e, o, left(e), pad], axis=0).astype(BF)

    repeat(p.zd, U_STACK, stack)
    tail = p.zd * p.sx
    se[tail:, :] = jnp.zeros((se.shape[0] - tail, nh), BF)
    so[tail:, :] = jnp.zeros((so.shape[0] - tail, nh), BF)

    r1 = p.x1 * cf
    ready(9 + 0, 9 + 12)
    b_first, b_second = rows(0, cf), rows(cf, cf)
    b_third, b_fourth = rows(2 * cf, cc), rows(2 * cf + cc, cc)
    b_fifth, b_sixth = rows(2 * cf + 2 * cc, cf), rows(3 * cf + 2 * cc, cf)

    def first(z):
        at = pl.ds(pl.multiple_of(z * p.sx, 16), p.k1)
        to = pl.ds(pl.multiple_of(z * r1, 16), r1)
        m1[to, :nh] = act(dot(a1[...], se[at, :]), b_first, cf)
        m1[to, nh:] = act(dot(a1[...], so[at, :]), b_first, cf)

    repeat(p.z1, U_FIRST, first)

    rp = p.xp * cf
    rs = p.xs * cf
    lead = (p.x2 - p.xs) // 2

    ready(9 + 1, 9 + 2)

    def keep(z, s, even, odd):
        lo, hi = max(s, lead), min(s + even.shape[0] // cf, lead + p.xs)
        if lo < hi:
            src = slice((lo - s) * cf, (hi - s) * cf)
            to = pl.ds(pl.multiple_of(z * rs + (lo - lead) * cf, 16), (hi - lo) * cf)
            sk[to, :nh] = even[src]
            sk[to, nh:] = odd[src]

    def pairs(even, odd):
        t = even.astype(F32) + odd.astype(F32)
        t = t.reshape(t.shape[0] // (2 * cf), 2, cf, nh)
        return t[:, 0] + t[:, 1]

    def pool(zz, s, total):
        n = total.shape[0] * cf
        pooled = (0.125 * total).reshape(n, nh).astype(BF)
        po[pl.ds(pl.multiple_of(zz * rp + s // 2 * cf, 16), n), :] = pooled

    def second(zz):
        for s in range(0, p.n2 * GROUP, GROUP):
            n = GROUP * cf
            total = None
            for dz in range(2):
                base = (2 * zz + dz) * r1 + s * cf
                k = (GROUP + 2) * cf
                e = dot(a2[...], window(m1, base, r1, k, p.k2, 0))
                o = dot(a2[...], window(m1, base, r1, k, p.k2, nh))
                even, odd = taps(e, o, n)
                even = act(even, b_second, cf)
                odd = act(odd, b_second, cf)
                keep(2 * zz + dz, s, even, odd)
                t = pairs(even, odd)
                total = t if total is None else total + t
            pool(zz, s, total)
        if p.rest:
            s = p.n2 * GROUP
            n = p.rest * cf
            base = 2 * zz * r1 + s * cf
            k = (p.rest + 2) * cf
            e = dot(ar[...], window(m1, base, r1, k, p.kr, 0, 4))
            o = dot(ar[...], window(m1, base, r1, k, p.kr, nh, 4))
            even, odd = taps(e, o, 2 * n)
            even = act(even, b_second, cf)
            odd = act(odd, b_second, cf)
            keep(2 * zz, s, even[:n], odd[:n])
            keep(2 * zz + 1, s, even[n:], odd[n:])
            t = pairs(even, odd)
            pool(zz, s, t[: p.rest // 2] + t[p.rest // 2 :])

    repeat(p.zp, U_SECOND, second)
    tail = p.zp * rp
    po[tail:, :] = jnp.zeros((po.shape[0] - tail, nh), BF)

    r3 = p.x3 * cc

    def third(z):
        v = dot(a3[...], po[pl.ds(pl.multiple_of(z * rp, 16), p.k3), :])
        v = right(v[:r3]) + v[r3 : 2 * r3] + left(v[2 * r3 :])
        c1[pl.ds(pl.multiple_of(z * r3, 16), r3), :] = act(v, b_third, cc)

    ready(9 + 3)
    repeat(p.z3, U_THIRD, third)
    r4 = p.x4 * cc

    def fourth(z):
        v = dot(a4[...], window(c1, z * r3, r3, r3, p.k4, 0))
        v = right(v[:r4]) + v[r4 : 2 * r4] + left(v[2 * r4 :])
        c2[pl.ds(pl.multiple_of(z * r4, 16), r4), :] = act(v, b_fourth, cc)

    ready(9 + 4)
    repeat(p.z4, U_FOURTH, fourth)
    tail = p.z4 * r4
    c2[tail:, :] = jnp.zeros((c2.shape[0] - tail, nh), BF)
    r5 = p.x5 * cf
    skip_lead = (p.z2 - p.zs) // 2

    def fifth(pair):
        for odd_z in range(2):
            z = 2 * pair + odd_z
            ac = ac0 if odd_z else ac1
            q = dot(ac[...], c2[pl.ds(pl.multiple_of(pair * r4, 16), p.kc), :])
            q0, q1, q2 = q[:r5], q[r5 : 2 * r5], q[2 * r5 :]
            done = 0
            e3 = [[], [], []]
            o3 = [[], [], []]
            n = p.g5 * cf
            for s in p.s5:
                rows = (p.g5 + 2) * cf
                base = (z + skip_lead) * rs + s * cf
                e = dot(a5[...], window(sk, base, rs, rows, p.k5, 0))
                o = dot(a5[...], window(sk, base, rs, rows, p.k5, nh))
                new = (done - s) * cf
                for dy in range(3):
                    e3[dy].append(e[dy * n + new : (dy + 1) * n])
                    o3[dy].append(o[dy * n + new : (dy + 1) * n])
                done = s + p.g5
            e0, e1, e2 = (jnp.concatenate(v, axis=0) for v in e3)
            o0, o1, o2 = (jnp.concatenate(v, axis=0) for v in o3)
            even = right(o0 + q0) + (e1 + o2 + (q1 + q2))
            odd = (e0 + o1 + (q0 + q1)) + left(e2 + q2)
            to = pl.ds(pl.multiple_of(z * r5, 16), r5)
            de[to, :nh] = act(even, b_fifth, cf)
            de[to, nh:] = act(odd, b_fifth, cf)

    ready(9 + 5, 9 + 6, 9 + 7)
    repeat(p.z5 // 2, U_FIFTH, fifth)
    tail = p.z5 * r5
    de[tail:, :] = jnp.zeros((de.shape[0] - tail, p.ny), BF)
    r6 = p.xl * cf

    def sixth(z):
        at = pl.ds(pl.multiple_of(z * r5, 16), p.k6)
        e = dot(a6[...], de[at, :nh])
        o = dot(a6[...], de[at, nh:])
        even, odd = taps(e, o, r6)
        to = pl.ds(pl.multiple_of(z * r6, 16), r6)
        rf[to, :nh] = act(even, b_sixth, cf)
        rf[to, nh:] = act(odd, b_sixth, cf)

    ready(9 + 8)
    repeat(p.zl, U_SIXTH, sixth)
    last = 4 * cf + 2 * cc
    ready(9 + 9, 9 + 11)
    field = dot(hd[...], rf[...]) + bias[last : last + 1, 0:1]
    high = field.astype(BF)
    low = (field - high.astype(F32)).astype(BF)
    both = jnp.concatenate([high, low], axis=0)
    for k in range(p.ny // span):
        at = slice(k * LANES, (k + 1) * LANES)
        v = jnp.concatenate([both[:, at], both[:, nh + k * LANES : nh + (k + 1) * LANES]], axis=1)
        v = dot(v, pt[...])
        out[:, k * span : (k + 1) * span] = v[: p.cells] + v[p.cells :]


def shift(block, axis, step):
    count = lax.axis_size(axis)
    return lax.ppermute(block, axis, [((i + step) % count, i) for i in range(count)])


def body(
    density,
    w_first,
    b_first,
    w_second,
    b_second,
    w_third,
    b_third,
    w_fourth,
    b_fourth,
    w_fifth,
    b_fifth,
    w_sixth,
    b_sixth,
    w_head,
    b_head,
):
    zl, xl, ny = density.shape
    cf, cc = w_second.shape[0], w_third.shape[0]
    h = HALO
    p = Plan(zl, xl, ny, cf, cc)

    left = shift(density[:, xl - h :], "tile", -1)
    right = shift(density[:, :h], "tile", 1)
    columns = [left, density, right]
    below = [shift(c[zl - h :], "gz", -1) for c in columns]
    above = [shift(c[:h], "gz", 1) for c in columns]
    blocks = [b.reshape(-1, ny) for b in below + columns + above]

    def taps(w, *last):
        return w.transpose(2, 3, 4, *last).reshape(-1, w.shape[last[1]])

    weights = [taps(w, 0, 1) for w in (w_second, w_sixth, w_fifth, w_fourth)]
    weights += [taps(w_third, 1, 0), w_first[:, 0].transpose(1, 2, 3, 0), w_head[None]]
    biases = [b_first, b_second, b_third, b_fourth, b_fifth, b_sixth, b_head]
    tabs = p.tables()
    widths = [t.shape[1] for t in tabs]
    tab = jnp.asarray(np.concatenate(tabs, axis=1))
    bias_rows = sum(up(b.shape[0], 8) for b in biases)

    sds = jax.ShapeDtypeStruct
    mats = [
        sds((p.x1 * cf, p.k1), BF),
        sds((3 * GROUP * cf, p.k2), BF),
        sds((max(6 * p.rest * cf, 16), p.kr), BF),
        sds((3 * p.x3 * cc, p.k3), BF),
        sds((3 * p.x4 * cc, p.k4), BF),
        sds((3 * p.g5 * cf, p.k5), BF),
        sds((3 * p.x5 * cf, p.kc), BF),
        sds((3 * p.x5 * cf, p.kc), BF),
        sds((3 * p.xl * cf, p.k6), BF),
        sds((p.cells, p.cells * cf), BF),
        sds((p.span, p.span), BF),
        sds((p.span, p.span), BF),
        sds((bias_rows, p.nh), F32),
    ]
    vmem = pl.BlockSpec(memory_space=pltpu.VMEM)
    smem = pl.BlockSpec(memory_space=pltpu.SMEM)
    anym = pl.BlockSpec(memory_space=pl.ANY)
    tables = pl.pallas_call(
        lambda *refs: prep_kernel(p, widths, *refs),
        in_specs=[vmem] * 8 + [smem] * 7,
        out_specs=[vmem] * MATS,
        out_shape=mats,
        scratch_shapes=[pltpu.VMEM((72, LANES), F32)],
        name="bands",
    )(tab, *weights, *biases)

    rows = sum(b.shape[0] for b in blocks)
    field = pl.pallas_call(
        lambda *refs: main_kernel(p, *refs),
        in_specs=[anym] * (9 + MATS),
        out_specs=vmem,
        out_shape=sds((p.cells, ny), F32),
        scratch_shapes=[
            pltpu.VMEM((p.zd, p.xd, ny), F32),
            pltpu.VMEM((p.zd * p.sx + 256, p.nh), BF),
            pltpu.VMEM((p.zd * p.sx + 256, p.nh), BF),
            pltpu.VMEM((p.z1 * p.x1 * cf, ny), BF),
            pltpu.VMEM((p.z2 * p.xs * cf, ny), BF),
            pltpu.VMEM((p.zp * p.xp * cf + 256, p.nh), BF),
            pltpu.VMEM((p.z3 * p.x3 * cc, p.nh), BF),
            pltpu.VMEM((p.z4 * p.x4 * cc + 256, p.nh), BF),
            pltpu.VMEM((p.z5 * p.x5 * cf + 256, ny), BF),
            pltpu.VMEM((p.cells * cf, ny), BF),
            pltpu.VMEM((rows, ny), BF),
        ]
        + [pltpu.VMEM(m.shape, m.dtype) for m in mats]
        + [pltpu.SemaphoreType.DMA((9 + MATS,))],
        name="unet",
    )(*blocks, *tables)
    return field.reshape(zl, xl, ny)


def solution(mesh):
    return jax.shard_map(
        body,
        mesh=mesh,
        in_specs=(P("gz", "tile", None),) + (P(),) * 14,
        out_specs=P("gz", "tile", None),
        check_vma=False,
    )
```

time: 38.6 us -> 31 us (0.80)
  Pallas kernels: 20.1 us -> 15 us
  local copies, waits for them, and re-layouts: 5.38 us -> 0.67 us
  starting transfers between devices: 10.7 us -> 12.7 us
  waiting for transfers between devices: 0.02 us -> 1.73 us
  other arithmetic: 1.02 us -> 0 us
    pallas_call x1, Pallas kernels: 17.3 us -> 12 us  [body(): pl.pallas_call(lambda *refs: main_kernel(p, *refs), in_specs=[anym] * (9...]
    reshape x4 -> x0, local copies, waits for them, and re-layouts: 2.22 us -> none  [the longest x2 1.44 us: table(): return w.transpose(3, 4, 0, 2, 1).reshape(9 * w.shape[0], 3 * w.shape[1])]
    ppermute x8, starting transfers between devices: 10.7 us -> 12.7 us  [shift(): lax.ppermute(block, axis, [((i + step) % count, i) for i in range(count)])]
    ppermute x8, waiting for transfers between devices: 0.02 us -> 1.73 us  [shift(): lax.ppermute(block, axis, [((i + step) % count, i) for i in range(count)])]
    transpose x2 -> x0, other arithmetic: 1.02 us -> none  [table(): return w.transpose(3, 4, 0, 2, 1).reshape(9 * w.shape[0], 3 * w.shape[1])]
    transpose x3 -> x0, local copies, waits for them, and re-layouts: 0.83 us -> none  [the longest x1 0.74 us: body(): w1 = w_first[:, 0].transpose(2, 0, 1, 3).reshape(3 * cf, 9)]
    broadcast_in_dim x1 -> x0, local copies, waits for them, and re-layouts: 0.71 us -> none  [body(): bias = jnp.broadcast_to(biases[:, None], (biases.shape[0], p.nh))]
    another operation x3 -> x0, local copies, waits for them, and re-layouts: 0.68 us -> none  [the longest x2 0.67 us: body(): wh = jnp.tile(w_head.astype(F32), p.cells)[None]]
  transfers between devices with their start and end apart: 8 -> 8, of which waited for: 0 -> 1; matrix products, arithmetic and copies ran while one was open for 13% -> 0% of each run, Pallas kernels for 7% -> 10%
where the time goes in v1:
time: 31 us; the launch traced here: 30.8 us
  Pallas kernels  15 us (48%)
  starting transfers between devices  12.7 us (41%)
  waiting for transfers between devices  1.73 us (6%)
  between operations  0.76 us (2%)
  local copies, waits for them, and re-layouts  0.67 us (2%)
    ppermute x8, starting transfers between devices, shift(): lax.ppermute(block, axis, [((i + step) % count, i) for i in range(count)])  12.7 us
    pallas_call x1, Pallas kernels, body(): pl.pallas_call(lambda *refs: main_kernel(p, *refs), in_specs=[anym] * (9...  12 us
    pallas_call x1, Pallas kernels, body(): pl.pallas_call(lambda *refs: prep_kernel(p, widths, *refs), in_specs=[vme...  2.98 us
    ppermute x8, waiting for transfers between devices, shift(): lax.ppermute(block, axis, [((i + step) % count, i) for i in range(count)])  1.73 us
    unnamed x16, local copies, waits for them, and re-layouts  0.67 us
  transfers between devices with their start and end apart: 8, of which 1 were waited for; matrix products, arithmetic and copies ran while one was open for 0% of the time, Pallas kernels for 10%

profile of v1, /device:TPU:1, one launch (start us, length us, event | category | flops | bytes accessed | tf_op | source)
XLA Modules:
  0.0 30.8 jit_solution(10220080170076861603)
XLA Ops:
  0.0 5.1 %collective-permute-start.3 = (bf16[8,8,512]{2,1,0:T(8,128)(2,1)}, bf16[8,8,512]{2,1,0:T(8,128)(2,1)S(1)}, u32[]{:S(2)}, u32[]{:S(2)}) collective-permute-start(bf16[8,8,512]{2,1,0:T(8,128)(2,1)} %param.16), channel_id=1, source_target_pairs={{1,0},{2,1},{3,2},{4,3},{5,4},{6,5},{7,6},{0,7},{9,8},{10,9},{11,1... | collective-permute-start | bytes 196616 | tf_op jit(solution)/shard_map/ppermute | solution.py:471
  5.1 0.0 collective-permute-start
  5.1 2.1 %collective-permute-start.2 = (bf16[8,8,512]{2,1,0:T(8,128)(2,1)}, bf16[8,8,512]{2,1,0:T(8,128)(2,1)S(1)}, u32[]{:S(2)}, u32[]{:S(2)}) collective-permute-start(bf16[8,8,512]{2,1,0:T(8,128)(2,1)} %param.16), channel_id=1, source_target_pairs={{24,0},{0,8},{8,16},{16,24},{25,1},{1,9},{9,17},{17,25},{26,2},{2,... | collective-permute-start | bytes 196616 | tf_op jit(solution)/shard_map/ppermute | solution.py:471
  7.2 0.0 collective-permute-start.6
  7.2 0.0 collective-permute-done.3
  7.2 0.0 copy-start
  7.2 1.1 %collective-permute-start.7 = (bf16[8,8,512]{2,1,0:T(8,128)(2,1)S(1)}, bf16[8,8,512]{2,1,0:T(8,128)(2,1)S(1)}, u32[]{:S(2)}, u32[]{:S(2)}) collective-permute-start(bf16[8,8,512]{2,1,0:T(8,128)(2,1)S(1)} %collective-permute-done.3), channel_id=1, source_target_pairs={{8,0},{16,8},{24,16},{0,24},{9,1},{17,9},{25,17},{1,25},{10,2},{18... | collective-permute-start | bytes 196616 | tf_op jit(solution)/shard_map/ppermute | solution.py:471
  8.2 1.1 %collective-permute-start.4 = (bf16[8,8,512]{2,1,0:T(8,128)(2,1)S(1)}, bf16[8,8,512]{2,1,0:T(8,128)(2,1)S(1)}, u32[]{:S(2)}, u32[]{:S(2)}) collective-permute-start(bf16[8,8,512]{2,1,0:T(8,128)(2,1)S(1)} %collective-permute-done.3), channel_id=1, source_target_pairs={{24,0},{0,8},{8,16},{16,24},{25,1},{1,9},{9,17},{17,25},{26,2},{2,... | collective-permute-start | bytes 196616 | tf_op jit(solution)/shard_map/ppermute | solution.py:471
  9.4 1.7 %collective-permute-done = bf16[8,8,512]{2,1,0:T(8,128)(2,1)S(1)} collective-permute-done((bf16[8,8,512]{2,1,0:T(8,128)(2,1)}, bf16[8,8,512]{2,1,0:T(8,128)(2,1)S(1)}, u32[]{:S(2)}, u32[]{:S(2)}) %collective-permute-start) | collective-permute-done | bytes 65568 | tf_op jit(solution)/shard_map/ppermute | solution.py:471
  11.1 2.1 %collective-permute-start.5 = (bf16[8,8,512]{2,1,0:T(8,128)(2,1)S(1)}, bf16[8,8,512]{2,1,0:T(8,128)(2,1)S(1)}, u32[]{:S(2)}, u32[]{:S(2)}) collective-permute-start(bf16[8,8,512]{2,1,0:T(8,128)(2,1)S(1)} %collective-permute-done), channel_id=1, source_target_pairs={{8,0},{16,8},{24,16},{0,24},{9,1},{17,9},{25,17},{1,25},{10,2},{18... | collective-permute-start | bytes 196616 | tf_op jit(solution)/shard_map/ppermute | solution.py:471
  13.2 0.0 collective-permute-done.2
  13.2 1.2 %collective-permute-start.1 = (bf16[8,8,512]{2,1,0:T(8,128)(2,1)S(1)}, bf16[8,8,512]{2,1,0:T(8,128)(2,1)S(1)}, u32[]{:S(2)}, u32[]{:S(2)}) collective-permute-start(bf16[8,8,512]{2,1,0:T(8,128)(2,1)S(1)} %collective-permute-done), channel_id=1, source_target_pairs={{24,0},{0,8},{8,16},{16,24},{25,1},{1,9},{9,17},{17,25},{26,2},{2,... | collective-permute-start | bytes 196616 | tf_op jit(solution)/shard_map/ppermute | solution.py:471
  15.0 3.0 %bands.1 = (bf16[176,256]{1,0:T(8,128)(2,1)}, bf16[192,256]{1,0:T(8,128)(2,1)}, bf16[192,256]{1,0:T(8,128)(2,1)}, bf16[384,256]{1,0:T(8,128)(2,1)}, bf16[288,384...) custom-call(s32[3,3200]{1,0:T(4,128)} %constant.2.clone.refs_0_, ...), custom_call_target="tpu_custom_call" | custom-call | tf_op jit(solution)/shard_map/bands/pallas_call | solution.py:533
  18.0 0.0 copy-done
  18.0 0.0 copy-done.1
  18.0 0.0 copy-done.2
  18.1 0.0 collective-permute-done.6
  18.1 0.0 copy-start.3
  18.1 0.0 collective-permute-done.7
  18.1 0.0 copy-start.4
  18.1 0.0 collective-permute-done.4
  18.1 0.0 copy-start.5
  18.1 0.0 collective-permute-done.5
  18.1 0.0 copy-start.6
  18.1 0.0 collective-permute-done.1
  18.1 0.0 copy-start.7
  18.2 0.5 %copy-done.3 = bf16[8,8,512]{2,1,0:T(8,128)(2,1)} copy-done((bf16[8,8,512]{2,1,0:T(8,128)(2,1)}, bf16[8,8,512]{2,1,0:T(8,128)(2,1)S(1)}, u32[]{:S(2)}) %copy-start.3) | copy-done | bytes 65560
  18.7 0.0 copy-done.4
  18.7 0.0 copy-done.5
  18.7 0.0 copy-done.6
  18.8 0.0 copy-done.7
  18.8 12.0 %unet.1 = f32[64,512]{1,0:T(8,128)} custom-call(bf16[64,512]{1,0:T(8,128)(2,1)} %bitcast.38, bf16[64,512]{1,0:T(8,128)(2,1)} %bitcast.33, bf16[64,512]{1,0:T(8,128)(2,1)} %bitcast.36, bf16[64,512]{1,0:T(8,128)(2,1)} %bitcast.32, bf16[64,512]{1,0:T(8,128)(2,1)} %bitcast.30, bf16[64,512]{1,0:T(8,128)(2,1)} %bitcast.31, bf16[64,512]{1,0:T(8,128)(2,1)} %bitcast.37, ...), custom_call_target="tpu_custom_call" | custom-call | tf_op jit(solution)/shard_map/unet/pallas_call | solution.py:543
  (2 shorter events, 0.0 us)
Async XLA Ops:
  0.0 7.2 %collective-permute-start.3 = (bf16[8,8,512]{2,1,0:T(8,128)(2,1)}, bf16[8,8,512]{2,1,0:T(8,128)(2,1)S(1)}, u32[]{:S(2)}, u32[]{:S(2)}) collective-permute-start(bf16[8,8,512]{2,1,0:T(8,128)(2,1)} %param.16), channel_id=1, source_target_pairs={{1,0},{2,1},{3,2},{4,3},{5,4},{6,5},{7,6},{0,7},{9,8},{10,9},{11,1... | collective-permute-start | bytes 196616 | tf_op jit(solution)/shard_map/ppermute | solution.py:471
  5.1 6.0 %collective-permute-start = (bf16[8,8,512]{2,1,0:T(8,128)(2,1)}, bf16[8,8,512]{2,1,0:T(8,128)(2,1)S(1)}, u32[]{:S(2)}, u32[]{:S(2)}) collective-permute-start(bf16[8,8,512]{2,1,0:T(8,128)(2,1)} %param.16), channel_id=1, source_target_pairs={{7,0},{0,1},{1,2},{2,3},{3,4},{4,5},{5,6},{6,7},{15,8},{8,9},{9,10... | collective-permute-start | bytes 196616 | tf_op jit(solution)/shard_map/ppermute | solution.py:471
  5.1 8.1 %collective-permute-start.2 = (bf16[8,8,512]{2,1,0:T(8,128)(2,1)}, bf16[8,8,512]{2,1,0:T(8,128)(2,1)S(1)}, u32[]{:S(2)}, u32[]{:S(2)}) collective-permute-start(bf16[8,8,512]{2,1,0:T(8,128)(2,1)} %param.16), channel_id=1, source_target_pairs={{24,0},{0,8},{8,16},{16,24},{25,1},{1,9},{9,17},{17,25},{26,2},{2,... | collective-permute-start | bytes 196616 | tf_op jit(solution)/shard_map/ppermute | solution.py:471
  7.2 10.9 %collective-permute-start.6 = (bf16[8,8,512]{2,1,0:T(8,128)(2,1)}, bf16[8,8,512]{2,1,0:T(8,128)(2,1)S(1)}, u32[]{:S(2)}, u32[]{:S(2)}) collective-permute-start(bf16[8,8,512]{2,1,0:T(8,128)(2,1)} %param.16), channel_id=1, source_target_pairs={{8,0},{16,8},{24,16},{0,24},{9,1},{17,9},{25,17},{1,25},{10,2},{18... | collective-permute-start | bytes 196616 | tf_op jit(solution)/shard_map/ppermute | solution.py:471
  7.2 10.9 %copy-start = (bf16[8,8,512]{2,1,0:T(8,128)(2,1)}, bf16[8,8,512]{2,1,0:T(8,128)(2,1)S(1)}, u32[]{:S(2)}) copy-start(bf16[8,8,512]{2,1,0:T(8,128)(2,1)S(1)} %collective-permute-done.3) | copy-start | bytes 196612
  7.2 10.9 %collective-permute-start.7 = (bf16[8,8,512]{2,1,0:T(8,128)(2,1)S(1)}, bf16[8,8,512]{2,1,0:T(8,128)(2,1)S(1)}, u32[]{:S(2)}, u32[]{:S(2)}) collective-permute-start(bf16[8,8,512]{2,1,0:T(8,128)(2,1)S(1)} %collective-permute-done.3), channel_id=1, source_target_pairs={{8,0},{16,8},{24,16},{0,24},{9,1},{17,9},{25,17},{1,25},{10,2},{18... | collective-permute-start | bytes 196616 | tf_op jit(solution)/shard_map/ppermute | solution.py:471
  8.2 9.9 %collective-permute-start.4 = (bf16[8,8,512]{2,1,0:T(8,128)(2,1)S(1)}, bf16[8,8,512]{2,1,0:T(8,128)(2,1)S(1)}, u32[]{:S(2)}, u32[]{:S(2)}) collective-permute-start(bf16[8,8,512]{2,1,0:T(8,128)(2,1)S(1)} %collective-permute-done.3), channel_id=1, source_target_pairs={{24,0},{0,8},{8,16},{16,24},{25,1},{1,9},{9,17},{17,25},{26,2},{2,... | collective-permute-start | bytes 196616 | tf_op jit(solution)/shard_map/ppermute | solution.py:471
  11.1 6.9 %copy-start.1 = (bf16[8,8,512]{2,1,0:T(8,128)(2,1)}, bf16[8,8,512]{2,1,0:T(8,128)(2,1)S(1)}, u32[]{:S(2)}) copy-start(bf16[8,8,512]{2,1,0:T(8,128)(2,1)S(1)} %collective-permute-done) | copy-start | bytes 196612
  11.1 7.0 %collective-permute-start.5 = (bf16[8,8,512]{2,1,0:T(8,128)(2,1)S(1)}, bf16[8,8,512]{2,1,0:T(8,128)(2,1)S(1)}, u32[]{:S(2)}, u32[]{:S(2)}) collective-permute-start(bf16[8,8,512]{2,1,0:T(8,128)(2,1)S(1)} %collective-permute-done), channel_id=1, source_target_pairs={{8,0},{16,8},{24,16},{0,24},{9,1},{17,9},{25,17},{1,25},{10,2},{18... | collective-permute-start | bytes 196616 | tf_op jit(solution)/shard_map/ppermute | solution.py:471
  13.2 4.8 %copy-start.2 = (bf16[8,8,512]{2,1,0:T(8,128)(2,1)}, bf16[8,8,512]{2,1,0:T(8,128)(2,1)S(1)}, u32[]{:S(2)}) copy-start(bf16[8,8,512]{2,1,0:T(8,128)(2,1)S(1)} %collective-permute-done.2) | copy-start | bytes 196612
  13.2 4.9 %collective-permute-start.1 = (bf16[8,8,512]{2,1,0:T(8,128)(2,1)S(1)}, bf16[8,8,512]{2,1,0:T(8,128)(2,1)S(1)}, u32[]{:S(2)}, u32[]{:S(2)}) collective-permute-start(bf16[8,8,512]{2,1,0:T(8,128)(2,1)S(1)} %collective-permute-done), channel_id=1, source_target_pairs={{24,0},{0,8},{8,16},{16,24},{25,1},{1,9},{9,17},{17,25},{26,2},{2,... | collective-permute-start | bytes 196616 | tf_op jit(solution)/shard_map/ppermute | solution.py:471
  18.1 0.6 %copy-start.3 = (bf16[8,8,512]{2,1,0:T(8,128)(2,1)}, bf16[8,8,512]{2,1,0:T(8,128)(2,1)S(1)}, u32[]{:S(2)}) copy-start(bf16[8,8,512]{2,1,0:T(8,128)(2,1)S(1)} %collective-permute-done.6) | copy-start | bytes 196612
  18.1 0.6 %copy-start.4 = (bf16[8,8,512]{2,1,0:T(8,128)(2,1)}, bf16[8,8,512]{2,1,0:T(8,128)(2,1)S(1)}, u32[]{:S(2)}) copy-start(bf16[8,8,512]{2,1,0:T(8,128)(2,1)S(1)} %collective-permute-done.7) | copy-start | bytes 196612
  18.1 0.6 %copy-start.5 = (bf16[8,8,512]{2,1,0:T(8,128)(2,1)}, bf16[8,8,512]{2,1,0:T(8,128)(2,1)S(1)}, u32[]{:S(2)}) copy-start(bf16[8,8,512]{2,1,0:T(8,128)(2,1)S(1)} %collective-permute-done.4) | copy-start | bytes 196612
  18.1 0.6 %copy-start.6 = (bf16[8,8,512]{2,1,0:T(8,128)(2,1)}, bf16[8,8,512]{2,1,0:T(8,128)(2,1)S(1)}, u32[]{:S(2)}) copy-start(bf16[8,8,512]{2,1,0:T(8,128)(2,1)S(1)} %collective-permute-done.5) | copy-start | bytes 196612
  18.1 0.7 %copy-start.7 = (bf16[8,8,512]{2,1,0:T(8,128)(2,1)}, bf16[8,8,512]{2,1,0:T(8,128)(2,1)S(1)}, u32[]{:S(2)}) copy-start(bf16[8,8,512]{2,1,0:T(8,128)(2,1)S(1)} %collective-permute-done.1) | copy-start | bytes 196612

commit v2 on v1

--- a/solution.py
+++ b/solution.py
@@ -13,9 +13,8 @@
 GROUP = 8
 GROUP5 = 6
 LANES = 128
-U_STACK, U_FIRST, U_SECOND, U_THIRD, U_FOURTH, U_FIFTH, U_SIXTH = 6, 11, 2, 8, 6, 5, 8
+U_STACK, U_FIRST, U_SECOND, U_THIRD, U_FOURTH, U_FIFTH, U_SIXTH = 24, 22, 10, 8, 6, 5, 8
 MATS = 13
-ORDER = (10, 12, 0, 1, 2, 3, 4, 5, 6, 7, 8, 9, 11)
 CODE = 64
 
 
@@ -110,8 +109,8 @@
 
 
 def prep_kernel(plan, widths, *refs):
-    (tab, w2, w6, w5, w4, w3, w1, wh) = refs[:8]
-    biases = refs[8:15]
+    (tab, w2, w6, w5, w4, w3, w1, wh, bh) = refs[:9]
+    biases = refs[9:15]
     (a1, a2, ar, a3, a4, a5, ac0, ac1, a6, hd, pm, pt, bias) = refs[15:28]
     (t1,) = refs[28:]
     p = plan
@@ -209,6 +208,7 @@
             v = jnp.where(r == k, b[k], v)
         bias[at : at + m, :] = v
         at += m
+    bias[at : at + 8, :] = jnp.broadcast_to(bh[...], (8, p.nh))
 
 
 def repeat(n, unroll, body):
@@ -228,27 +228,10 @@
 
 def main_kernel(plan, *refs):
     p = plan
-    n = 9 + MATS
-    out = refs[n]
-    (dd, se, so, m1, sk, po, c1, c2, de, rf, raw) = refs[n + 1 : n + 12]
-    mats = refs[n + 12 : n + 12 + MATS]
-    sem = refs[n + 12 + MATS]
-    (a1, a2, ar, a3, a4, a5, ac0, ac1, a6, hd, pm, pt, bias) = mats
-    copies = []
-    row = 0
-    for k in range(9):
-        rows = refs[k].shape[0]
-        copies.append(pltpu.make_async_copy(refs[k], raw.at[pl.ds(row, rows)], sem.at[k]))
-        row += rows
-    for k in range(MATS):
-        copies.append(pltpu.make_async_copy(refs[9 + k], mats[k], sem.at[9 + k]))
-    for k in list(range(9)) + [9 + ORDER[k] for k in range(MATS)]:
-        copies[k].start()
-
-    def ready(*names):
-        for k in names:
-            copies[k].wait()
-
+    blocks = refs[:9]
+    (a1, a2, ar, a3, a4, a5, ac0, ac1, a6, hd, pm, pt, bias) = refs[9 : 9 + MATS]
+    out = refs[9 + MATS]
+    (dd, se, so, m1, sk, po, c1, c2, de, rf) = refs[10 + MATS :]
     cf, cc, nh = p.cf, p.cc, p.nh
 
     def rows(lo, n):
@@ -285,8 +268,8 @@
         return even, odd
 
     h = HALO
-    ready(*range(9), 9 + 10)
     span = p.span
+    raw = jnp.concatenate([b[...] for b in blocks], axis=0)
     split = [dot(raw[:, y : y + span], pm[...]) for y in range(0, p.ny, span)]
     row = 0
     for bz, nz in ((0, h), (h, p.zl), (h + p.zl, h)):
@@ -313,7 +296,6 @@
     so[tail:, :] = jnp.zeros((so.shape[0] - tail, nh), BF)
 
     r1 = p.x1 * cf
-    ready(9 + 0, 9 + 12)
     b_first, b_second = rows(0, cf), rows(cf, cf)
     b_third, b_fourth = rows(2 * cf, cc), rows(2 * cf + cc, cc)
     b_fifth, b_sixth = rows(2 * cf + 2 * cc, cf), rows(3 * cf + 2 * cc, cf)
@@ -330,7 +312,6 @@
     rs = p.xs * cf
     lead = (p.x2 - p.xs) // 2
 
-    ready(9 + 1, 9 + 2)
 
     def keep(z, s, even, odd):
         lo, hi = max(s, lead), min(s + even.shape[0] // cf, lead + p.xs)
@@ -392,7 +373,6 @@
         v = right(v[:r3]) + v[r3 : 2 * r3] + left(v[2 * r3 :])
         c1[pl.ds(pl.multiple_of(z * r3, 16), r3), :] = act(v, b_third, cc)
 
-    ready(9 + 3)
     repeat(p.z3, U_THIRD, third)
     r4 = p.x4 * cc
 
@@ -401,7 +381,6 @@
         v = right(v[:r4]) + v[r4 : 2 * r4] + left(v[2 * r4 :])
         c2[pl.ds(pl.multiple_of(z * r4, 16), r4), :] = act(v, b_fourth, cc)
 
-    ready(9 + 4)
     repeat(p.z4, U_FOURTH, fourth)
     tail = p.z4 * r4
     c2[tail:, :] = jnp.zeros((c2.shape[0] - tail, nh), BF)
@@ -436,7 +415,6 @@
             de[to, :nh] = act(even, b_fifth, cf)
             de[to, nh:] = act(odd, b_fifth, cf)
 
-    ready(9 + 5, 9 + 6, 9 + 7)
     repeat(p.z5 // 2, U_FIFTH, fifth)
     tail = p.z5 * r5
     de[tail:, :] = jnp.zeros((de.shape[0] - tail, p.ny), BF)
@@ -451,10 +429,8 @@
         rf[to, :nh] = act(even, b_sixth, cf)
         rf[to, nh:] = act(odd, b_sixth, cf)
 
-    ready(9 + 8)
     repeat(p.zl, U_SIXTH, sixth)
     last = 4 * cf + 2 * cc
-    ready(9 + 9, 9 + 11)
     field = dot(hd[...], rf[...]) + bias[last : last + 1, 0:1]
     high = field.astype(BF)
     low = (field - high.astype(F32)).astype(BF)
@@ -504,47 +480,47 @@
         return w.transpose(2, 3, 4, *last).reshape(-1, w.shape[last[1]])
 
     weights = [taps(w, 0, 1) for w in (w_second, w_sixth, w_fifth, w_fourth)]
-    weights += [taps(w_third, 1, 0), w_first[:, 0].transpose(1, 2, 3, 0), w_head[None]]
-    biases = [b_first, b_second, b_third, b_fourth, b_fifth, b_sixth, b_head]
+    weights += [taps(w_third, 1, 0), w_first[:, 0].transpose(1, 2, 3, 0), w_head[None], b_head[None]]
+    biases = [b_first, b_second, b_third, b_fourth, b_fifth, b_sixth]
     tabs = p.tables()
     widths = [t.shape[1] for t in tabs]
     tab = jnp.asarray(np.concatenate(tabs, axis=1))
-    bias_rows = sum(up(b.shape[0], 8) for b in biases)
-
-    sds = jax.ShapeDtypeStruct
+    bias_rows = sum(up(b.shape[0], 8) for b in biases + [b_head])
+
     mats = [
-        sds((p.x1 * cf, p.k1), BF),
-        sds((3 * GROUP * cf, p.k2), BF),
-        sds((max(6 * p.rest * cf, 16), p.kr), BF),
-        sds((3 * p.x3 * cc, p.k3), BF),
-        sds((3 * p.x4 * cc, p.k4), BF),
-        sds((3 * p.g5 * cf, p.k5), BF),
-        sds((3 * p.x5 * cf, p.kc), BF),
-        sds((3 * p.x5 * cf, p.kc), BF),
-        sds((3 * p.xl * cf, p.k6), BF),
-        sds((p.cells, p.cells * cf), BF),
-        sds((p.span, p.span), BF),
-        sds((p.span, p.span), BF),
-        sds((bias_rows, p.nh), F32),
+        pltpu.VMEM((p.x1 * cf, p.k1), BF),
+        pltpu.VMEM((3 * GROUP * cf, p.k2), BF),
+        pltpu.VMEM((max(6 * p.rest * cf, 16), p.kr), BF),
+        pltpu.VMEM((3 * p.x3 * cc, p.k3), BF),
+        pltpu.VMEM((3 * p.x4 * cc, p.k4), BF),
+        pltpu.VMEM((3 * p.g5 * cf, p.k5), BF),
+        pltpu.VMEM((3 * p.x5 * cf, p.kc), BF),
+        pltpu.VMEM((3 * p.x5 * cf, p.kc), BF),
+        pltpu.VMEM((3 * p.xl * cf, p.k6), BF),
+        pltpu.VMEM((p.cells, p.cells * cf), BF),
+        pltpu.VMEM((p.span, p.span), BF),
+        pltpu.VMEM((p.span, p.span), BF),
+        pltpu.VMEM((bias_rows, p.nh), F32),
     ]
     vmem = pl.BlockSpec(memory_space=pltpu.VMEM)
     smem = pl.BlockSpec(memory_space=pltpu.SMEM)
-    anym = pl.BlockSpec(memory_space=pl.ANY)
     tables = pl.pallas_call(
         lambda *refs: prep_kernel(p, widths, *refs),
-        in_specs=[vmem] * 8 + [smem] * 7,
+        in_specs=[vmem] * 9 + [smem] * 6,
         out_specs=[vmem] * MATS,
         out_shape=mats,
         scratch_shapes=[pltpu.VMEM((72, LANES), F32)],
         name="bands",
     )(tab, *weights, *biases)
 
-    rows = sum(b.shape[0] for b in blocks)
+    def on_chip(arrays):
+        return [pltpu.with_memory_space_constraint(v, pltpu.VMEM) for v in arrays]
+
     field = pl.pallas_call(
         lambda *refs: main_kernel(p, *refs),
-        in_specs=[anym] * (9 + MATS),
+        in_specs=[vmem] * (9 + MATS),
         out_specs=vmem,
-        out_shape=sds((p.cells, ny), F32),
+        out_shape=jax.ShapeDtypeStruct((p.cells, ny), F32),
         scratch_shapes=[
             pltpu.VMEM((p.zd, p.xd, ny), F32),
             pltpu.VMEM((p.zd * p.sx + 256, p.nh), BF),
@@ -556,12 +532,9 @@
             pltpu.VMEM((p.z4 * p.x4 * cc + 256, p.nh), BF),
             pltpu.VMEM((p.z5 * p.x5 * cf + 256, ny), BF),
             pltpu.VMEM((p.cells * cf, ny), BF),
-            pltpu.VMEM((rows, ny), BF),
-        ]
-        + [pltpu.VMEM(m.shape, m.dtype) for m in mats]
-        + [pltpu.SemaphoreType.DMA((9 + MATS,))],
+        ],
         name="unet",
-    )(*blocks, *tables)
+    )(*on_chip(blocks), *on_chip(tables))
     return field.reshape(zl, xl, ny)
 
 

time: 31 us -> 25.6 us (0.83); the launches traced: 30.8 us -> 25.1 us
  Pallas kernels: 15 us -> 10.1 us
  local copies, waits for them, and re-layouts: 0.67 us -> 0.01 us
    pallas_call x1, Pallas kernels: 12 us -> 7.96 us  [body(): pl.pallas_call(lambda *refs: main_kernel(p, *refs), in_specs=[vmem] * (9...]
    pallas_call x1, Pallas kernels: 2.98 us -> 2.11 us  [body(): pl.pallas_call(lambda *refs: prep_kernel(p, widths, *refs), in_specs=[vme...]
    unnamed x16 -> x2, local copies, waits for them, and re-layouts: 0.67 us -> 0.01 us
  transfers between devices with their start and end apart: 8 -> 8, of which waited for: 1 -> 1; matrix products, arithmetic and copies ran while one was open for 0% -> 0% of each run, Pallas kernels for 10% -> 8%
where the time goes in v2:
time: 25.6 us; the launch traced here: 25.1 us
  starting transfers between devices  12.6 us (49%)
  Pallas kernels  10.1 us (39%)
  waiting for transfers between devices  1.74 us (7%)
  between operations  0.72 us (3%)
    ppermute x8, starting transfers between devices, shift(): lax.ppermute(block, axis, [((i + step) % count, i) for i in range(count)])  12.6 us
    pallas_call x1, Pallas kernels, body(): pl.pallas_call(lambda *refs: main_kernel(p, *refs), in_specs=[vmem] * (9...  7.96 us
    pallas_call x1, Pallas kernels, body(): pl.pallas_call(lambda *refs: prep_kernel(p, widths, *refs), in_specs=[vme...  2.11 us
    ppermute x8, waiting for transfers between devices, shift(): lax.ppermute(block, axis, [((i + step) % count, i) for i in range(count)])  1.74 us
  transfers between devices with their start and end apart: 8, of which 1 were waited for; matrix products, arithmetic and copies ran while one was open for 0% of the time, Pallas kernels for 8%

profile of v2, /device:TPU:1, one launch (start us, length us, event | category | flops | bytes accessed | tf_op | source)
XLA Modules:
  0.0 25.1 jit_solution(10988415850204804600)
XLA Ops:
  0.0 5.1 %collective-permute-start.3 = (bf16[8,8,512]{2,1,0:T(8,128)(2,1)}, bf16[8,8,512]{2,1,0:T(8,128)(2,1)S(1)}, u32[]{:S(2)}, u32[]{:S(2)}) collective-permute-start(bf16[8,8,512]{2,1,0:T(8,128)(2,1)} %param.16), channel_id=1, source_target_pairs={{1,0},{2,1},{3,2},{4,3},{5,4},{6,5},{7,6},{0,7},{9,8},{10,9},{11,1... | collective-permute-start | bytes 196616 | tf_op jit(solution)/shard_map/ppermute | solution.py:447
  5.1 0.0 collective-permute-start
  5.1 2.1 %collective-permute-start.2 = (bf16[8,8,512]{2,1,0:T(8,128)(2,1)}, bf16[8,8,512]{2,1,0:T(8,128)(2,1)S(1)}, u32[]{:S(2)}, u32[]{:S(2)}) collective-permute-start(bf16[8,8,512]{2,1,0:T(8,128)(2,1)} %param.16), channel_id=1, source_target_pairs={{24,0},{0,8},{8,16},{16,24},{25,1},{1,9},{9,17},{17,25},{26,2},{2,... | collective-permute-start | bytes 196616 | tf_op jit(solution)/shard_map/ppermute | solution.py:447
  7.2 0.0 collective-permute-start.6
  7.2 0.0 collective-permute-done.3
  7.2 1.1 %collective-permute-start.7 = (bf16[8,8,512]{2,1,0:T(8,128)(2,1)S(1)}, bf16[8,8,512]{2,1,0:T(8,128)(2,1)S(1)}, u32[]{:S(2)}, u32[]{:S(2)}) collective-permute-start(bf16[8,8,512]{2,1,0:T(8,128)(2,1)S(1)} %collective-permute-done.3), channel_id=1, source_target_pairs={{8,0},{16,8},{24,16},{0,24},{9,1},{17,9},{25,17},{1,25},{10,2},{18... | collective-permute-start | bytes 196616 | tf_op jit(solution)/shard_map/ppermute | solution.py:447
  8.2 1.1 %collective-permute-start.4 = (bf16[8,8,512]{2,1,0:T(8,128)(2,1)S(1)}, bf16[8,8,512]{2,1,0:T(8,128)(2,1)S(1)}, u32[]{:S(2)}, u32[]{:S(2)}) collective-permute-start(bf16[8,8,512]{2,1,0:T(8,128)(2,1)S(1)} %collective-permute-done.3), channel_id=1, source_target_pairs={{24,0},{0,8},{8,16},{16,24},{25,1},{1,9},{9,17},{17,25},{26,2},{2,... | collective-permute-start | bytes 196616 | tf_op jit(solution)/shard_map/ppermute | solution.py:447
  9.4 1.7 %collective-permute-done = bf16[8,8,512]{2,1,0:T(8,128)(2,1)S(1)} collective-permute-done((bf16[8,8,512]{2,1,0:T(8,128)(2,1)}, bf16[8,8,512]{2,1,0:T(8,128)(2,1)S(1)}, u32[]{:S(2)}, u32[]{:S(2)}) %collective-permute-start) | collective-permute-done | bytes 65568 | tf_op jit(solution)/shard_map/ppermute | solution.py:447
  11.1 2.1 %collective-permute-start.5 = (bf16[8,8,512]{2,1,0:T(8,128)(2,1)S(1)}, bf16[8,8,512]{2,1,0:T(8,128)(2,1)S(1)}, u32[]{:S(2)}, u32[]{:S(2)}) collective-permute-start(bf16[8,8,512]{2,1,0:T(8,128)(2,1)S(1)} %collective-permute-done), channel_id=1, source_target_pairs={{8,0},{16,8},{24,16},{0,24},{9,1},{17,9},{25,17},{1,25},{10,2},{18... | collective-permute-start | bytes 196616 | tf_op jit(solution)/shard_map/ppermute | solution.py:447
  13.2 0.0 collective-permute-done.2
  13.2 1.1 %collective-permute-start.1 = (bf16[8,8,512]{2,1,0:T(8,128)(2,1)S(1)}, bf16[8,8,512]{2,1,0:T(8,128)(2,1)S(1)}, u32[]{:S(2)}, u32[]{:S(2)}) collective-permute-start(bf16[8,8,512]{2,1,0:T(8,128)(2,1)S(1)} %collective-permute-done), channel_id=1, source_target_pairs={{24,0},{0,8},{8,16},{16,24},{25,1},{1,9},{9,17},{17,25},{26,2},{2,... | collective-permute-start | bytes 196616 | tf_op jit(solution)/shard_map/ppermute | solution.py:447
  15.0 0.0 copy-start
  15.0 2.1 %bands.1 = (bf16[176,256]{1,0:T(8,128)(2,1)S(1)}, bf16[192,256]{1,0:T(8,128)(2,1)S(1)}, bf16[192,256]{1,0:T(8,128)(2,1)S(1)}, bf16[384,256]{1,0:T(8,128)(2,1)S(1...) custom-call(s32[3,3200]{1,0:T(4,128)} %constant.2.clone.refs_0_, ...), custom_call_target="tpu_custom_call" | custom-call | tf_op jit(solution)/shard_map/bands/pallas_call | solution.py:507
  17.1 0.0 collective-permute-done.6
  17.1 0.0 collective-permute-done.7
  17.1 0.0 collective-permute-done.4
  17.1 0.0 collective-permute-done.5
  17.2 0.0 collective-permute-done.1
  17.2 0.0 copy-done
  17.2 8.0 %unet.1 = f32[64,512]{1,0:T(8,128)} custom-call(bf16[64,512]{1,0:T(8,128)(2,1)S(1)} %bitcast.39, bf16[64,512]{1,0:T(8,128)(2,1)S(1)} %bitcast.34, bf16[64,512]{1,0:T(8,128)(2,1)S(1)} %bitcast.37, bf16[64,512]{1,0:T(8,128)(2,1)S(1)} %bitcast.33, bf16[64,512]{1,0:T(8,128)(2,1)S(1)} %bitcast.31, bf16[64,512]{1,0:T(8,128)(2,1)S(1)} %bitcast.32, ...), custom_call_target="tpu_custom_call" | custom-call | tf_op jit(solution)/shard_map/unet/pallas_call | solution.py:519
Async XLA Ops:
  0.0 7.2 %collective-permute-start.3 = (bf16[8,8,512]{2,1,0:T(8,128)(2,1)}, bf16[8,8,512]{2,1,0:T(8,128)(2,1)S(1)}, u32[]{:S(2)}, u32[]{:S(2)}) collective-permute-start(bf16[8,8,512]{2,1,0:T(8,128)(2,1)} %param.16), channel_id=1, source_target_pairs={{1,0},{2,1},{3,2},{4,3},{5,4},{6,5},{7,6},{0,7},{9,8},{10,9},{11,1... | collective-permute-start | bytes 196616 | tf_op jit(solution)/shard_map/ppermute | solution.py:447
  5.1 6.0 %collective-permute-start = (bf16[8,8,512]{2,1,0:T(8,128)(2,1)}, bf16[8,8,512]{2,1,0:T(8,128)(2,1)S(1)}, u32[]{:S(2)}, u32[]{:S(2)}) collective-permute-start(bf16[8,8,512]{2,1,0:T(8,128)(2,1)} %param.16), channel_id=1, source_target_pairs={{7,0},{0,1},{1,2},{2,3},{3,4},{4,5},{5,6},{6,7},{15,8},{8,9},{9,10... | collective-permute-start | bytes 196616 | tf_op jit(solution)/shard_map/ppermute | solution.py:447
  5.1 8.1 %collective-permute-start.2 = (bf16[8,8,512]{2,1,0:T(8,128)(2,1)}, bf16[8,8,512]{2,1,0:T(8,128)(2,1)S(1)}, u32[]{:S(2)}, u32[]{:S(2)}) collective-permute-start(bf16[8,8,512]{2,1,0:T(8,128)(2,1)} %param.16), channel_id=1, source_target_pairs={{24,0},{0,8},{8,16},{16,24},{25,1},{1,9},{9,17},{17,25},{26,2},{2,... | collective-permute-start | bytes 196616 | tf_op jit(solution)/shard_map/ppermute | solution.py:447
  7.2 10.0 %collective-permute-start.6 = (bf16[8,8,512]{2,1,0:T(8,128)(2,1)}, bf16[8,8,512]{2,1,0:T(8,128)(2,1)S(1)}, u32[]{:S(2)}, u32[]{:S(2)}) collective-permute-start(bf16[8,8,512]{2,1,0:T(8,128)(2,1)} %param.16), channel_id=1, source_target_pairs={{8,0},{16,8},{24,16},{0,24},{9,1},{17,9},{25,17},{1,25},{10,2},{18... | collective-permute-start | bytes 196616 | tf_op jit(solution)/shard_map/ppermute | solution.py:447
  7.2 10.0 %collective-permute-start.7 = (bf16[8,8,512]{2,1,0:T(8,128)(2,1)S(1)}, bf16[8,8,512]{2,1,0:T(8,128)(2,1)S(1)}, u32[]{:S(2)}, u32[]{:S(2)}) collective-permute-start(bf16[8,8,512]{2,1,0:T(8,128)(2,1)S(1)} %collective-permute-done.3), channel_id=1, source_target_pairs={{8,0},{16,8},{24,16},{0,24},{9,1},{17,9},{25,17},{1,25},{10,2},{18... | collective-permute-start | bytes 196616 | tf_op jit(solution)/shard_map/ppermute | solution.py:447
  8.2 8.9 %collective-permute-start.4 = (bf16[8,8,512]{2,1,0:T(8,128)(2,1)S(1)}, bf16[8,8,512]{2,1,0:T(8,128)(2,1)S(1)}, u32[]{:S(2)}, u32[]{:S(2)}) collective-permute-start(bf16[8,8,512]{2,1,0:T(8,128)(2,1)S(1)} %collective-permute-done.3), channel_id=1, source_target_pairs={{24,0},{0,8},{8,16},{16,24},{25,1},{1,9},{9,17},{17,25},{26,2},{2,... | collective-permute-start | bytes 196616 | tf_op jit(solution)/shard_map/ppermute | solution.py:447
  11.1 6.1 %collective-permute-start.5 = (bf16[8,8,512]{2,1,0:T(8,128)(2,1)S(1)}, bf16[8,8,512]{2,1,0:T(8,128)(2,1)S(1)}, u32[]{:S(2)}, u32[]{:S(2)}) collective-permute-start(bf16[8,8,512]{2,1,0:T(8,128)(2,1)S(1)} %collective-permute-done), channel_id=1, source_target_pairs={{8,0},{16,8},{24,16},{0,24},{9,1},{17,9},{25,17},{1,25},{10,2},{18... | collective-permute-start | bytes 196616 | tf_op jit(solution)/shard_map/ppermute | solution.py:447
  13.2 4.0 %collective-permute-start.1 = (bf16[8,8,512]{2,1,0:T(8,128)(2,1)S(1)}, bf16[8,8,512]{2,1,0:T(8,128)(2,1)S(1)}, u32[]{:S(2)}, u32[]{:S(2)}) collective-permute-start(bf16[8,8,512]{2,1,0:T(8,128)(2,1)S(1)} %collective-permute-done), channel_id=1, source_target_pairs={{24,0},{0,8},{8,16},{16,24},{25,1},{1,9},{9,17},{17,25},{26,2},{2,... | collective-permute-start | bytes 196616 | tf_op jit(solution)/shard_map/ppermute | solution.py:447
  15.0 2.2 %copy-start = (bf16[8,8,512]{2,1,0:T(8,128)(2,1)S(1)}, bf16[8,8,512]{2,1,0:T(8,128)(2,1)}, u32[]{:S(2)}) copy-start(bf16[8,8,512]{2,1,0:T(8,128)(2,1)} %param.16) | copy-start | bytes 196612

commit v3 on v2

v3 whole, which is shorter than its diff:
```python
import numpy as np
import jax
import jax.numpy as jnp
from jax import lax
from jax.experimental import pallas as pl
from jax.experimental.pallas import tpu as pltpu
from jax.sharding import PartitionSpec as P


BF = jnp.bfloat16
F32 = jnp.float32
HALO = 8
GROUP = 8
GROUP5 = 6
GROUP4 = 3
LANES = 128
MATS = 13
VMEM_LIMIT = 52 << 20
CODE = 64


def up(n, m):
    return -(-n // m) * m


def starts(total, size, step):
    size = min(size, total)
    assert (total - size) % step == 0
    s = list(range(0, total - size + 1, size))
    if s[-1] + size < total:
        s.append(total - size)
    return size, s


def lanes_of(dims, row_of, rows2_of, x_of, width):
    zs, xs, cs = dims
    t = np.full((3, width), -1, np.int32)
    for z in range(zs):
        for x in range(xs):
            for i in range(cs):
                c = (z * xs + x) * cs + i
                t[0, c] = row_of(z, x, i)
                t[1, c] = rows2_of(z, x, i)
                t[2, c] = x_of(z, x, i)
    return t


class Plan:
    def __init__(self, zl, xl, ny, cf, cc):
        h = HALO
        self.zl, self.xl, self.ny, self.cf, self.cc = zl, xl, ny, cf, cc
        self.nh = ny // 2
        self.zd, self.xd = zl + 2 * h, xl + 2 * h
        self.z1, self.x1 = self.zd - 2, self.xd - 2
        self.z2, self.x2 = self.zd - 4, self.xd - 4
        self.zp, self.xp = self.z2 // 2, self.x2 // 2
        self.z3, self.x3 = self.zp - 2, self.xp - 2
        self.z4, self.x4 = self.zp - 4, self.xp - 4
        self.zs, self.xs = zl + 4, xl + 4
        self.z5, self.x5 = zl + 2, xl + 2
        self.sx = up(3 * self.xd, 16)
        self.k1 = up(3 * self.sx, 128)
        self.n2 = self.x2 // GROUP
        self.rest = self.x2 - self.n2 * GROUP
        self.g4, self.s4 = starts(self.x4, GROUP4, 1)
        self.g5, self.s5 = starts(self.x5, GROUP5, 2)
        self.k2 = up(3 * (GROUP + 2) * cf, 128)
        self.kr = up(4 * (self.rest + 2) * cf, 128)
        self.k3 = up(3 * self.xp * cf, 128)
        self.k4 = up(3 * (self.g4 + 2) * cc, 128)
        self.k5 = up(3 * (self.g5 + 2) * cf, 128)
        self.kc = up(2 * self.x4 * cc, 128)
        self.k6 = up(3 * self.x5 * cf, 128)
        self.cells = zl * xl
        self.span = 2 * LANES

    def tables(self):
        cf, cc = self.cf, self.cc
        none = lambda z, x, i: -1
        xof = lambda z, x, i: x
        code = lambda z, x, i: CODE * z + i
        a2 = lanes_of((3, GROUP + 2, cf), code, none, xof, self.k2)
        r0 = lanes_of((4, self.rest + 2, cf), lambda z, x, i: CODE * z + i if z < 3 else -1, none, xof, self.kr)
        r1 = lanes_of((4, self.rest + 2, cf), lambda z, x, i: CODE * (z - 1) + i if z else -1, none, xof, self.kr)
        a6 = lanes_of((3, self.x5, cf), code, none, xof, self.k6)
        a5 = lanes_of((3, self.g5 + 2, cf), code, none, xof, self.k5)
        ce = lanes_of(
            (2, self.x4, cc),
            lambda z, x, i: CODE * z + cf + i,
            lambda z, x, i: CODE * 2 + cf + i if z == 1 else -1,
            xof,
            self.kc,
        )
        co = lanes_of(
            (2, self.x4, cc),
            lambda z, x, i: CODE * 2 * z + cf + i,
            lambda z, x, i: CODE + cf + i if z == 0 else -1,
            xof,
            self.kc,
        )
        b4 = lanes_of((3, self.g4 + 2, cc), code, none, xof, self.k4)
        b3 = lanes_of((3, self.xp, cf), lambda z, x, i: cf * z + i, none, xof, self.k3)
        f1 = np.full((3, self.k1), -1, np.int32)
        for z in range(3):
            for dy in range(3):
                for x in range(self.xd):
                    c = z * self.sx + dy * self.xd + x
                    f1[0, c] = z * 24 + dy
                    f1[2, c] = x
        hd = lanes_of((1, self.cells, cf), lambda z, x, i: i, none, xof, self.cells * cf)
        return [a2, r0, r1, a6, a5, ce, co, b4, b3, f1, hd]


def prep_kernel(plan, widths, *refs):
    (tab, w2, w6, w5, w4, w3, w1, wh) = refs[:8]
    biases = refs[8:14]
    block = refs[14]
    (a1, a2, ar, a3, a4, a5, ac0, ac1, a6, hd, pm, pt, bias) = refs[15 : 15 + MATS]
    own, t1, t3 = refs[15 + MATS :]
    own[...] = block[...]
    p = plan
    cf, cc = p.cf, p.cc
    off = np.concatenate([[0], np.cumsum(widths)]).tolist()

    def expand(w, i, j, co):
        lo, hi = off[i], off[j]
        rows = w.shape[1]
        r = lax.broadcasted_iota(jnp.int32, (rows, hi - lo), 0)
        total = None
        for dz in range(3):
            m = (r + CODE * dz == tab[0:1, lo:hi]) | (r + CODE * dz == tab[1:2, lo:hi])
            g = dot(w[dz * 9 * co : (dz + 1) * 9 * co, :], jnp.where(m, 1.0, 0.0).astype(BF))
            total = g if total is None else total + g
        return total

    def select(w, i, base):
        lo, hi = off[i], off[i + 1]
        r = lax.broadcasted_iota(jnp.int32, (w.shape[1], hi - lo), 0)
        m = (r - base == tab[0:1, lo:hi]) & (tab[0:1, lo:hi] >= 0)
        return dot(w, jnp.where(m, 1.0, 0.0).astype(BF))

    def band(pieces, i, pick, outs):
        xi = tab[2:3, off[i] : off[i + 1]]
        parts = []
        for xo in range(outs):
            sums = {}
            for dx in range(3):
                at = pick(xo, dx)
                sums[at] = sums[at] + pieces[dx] if at in sums else pieces[dx]
            v = 0.0
            for at, piece in sums.items():
                v = jnp.where(xi == at, piece, v)
            parts.append(v)
        return parts

    def rows_of(g, lo, width, dy, co):
        return [
            g[(dx * 3 + dy) * co : (dx * 3 + dy + 1) * co, lo : lo + width] for dx in range(3)
        ]

    def full(out, g, lo, i, pick, outs, co):
        parts = []
        for dy in range(3):
            parts += band(rows_of(g, lo, widths[i], dy, co), i, pick, outs)
        out[...] = jnp.concatenate(parts, axis=0).astype(BF)

    near = lambda xo, dx: xo + dx
    half = lambda xo, dx: (xo + dx) // 2
    t1[...] = jnp.zeros(t1.shape, F32)
    for k in range(9):
        t1[8 * k : 8 * k + 3, :cf] = w1[k // 3, k % 3].astype(F32)
    turned = t1[...].T[:cf].astype(BF)
    a1[...] = jnp.concatenate(
        band([select(turned, 9, 8 * dx) for dx in range(3)], 9, near, p.x1), axis=0
    ).astype(BF)
    g = expand(w2, 0, 3, cf)
    full(a2, g, 0, 0, near, GROUP, cf)
    parts = []
    for dy in range(3):
        for zo in range(2):
            lo = off[1 + zo]
            parts += band(rows_of(g, lo, p.kr, dy, cf), 1 + zo, near, p.rest)
    if parts:
        ar[...] = jnp.concatenate(parts, axis=0).astype(BF)
    full(a6, expand(w6, 3, 4, cf), 0, 3, near, p.xl, cf)
    g = expand(w5, 4, 7, cf)
    full(a5, g, 0, 4, near, p.g5, cf)
    full(ac0, g, off[5] - off[4], 5, half, p.x5, cf)
    full(ac1, g, off[6] - off[4], 6, half, p.x5, cf)
    full(a4, expand(w4, 7, 8, cc), 0, 7, near, p.g4, cc)
    t3[...] = jnp.zeros(t3.shape, F32)
    for k in range(27):
        dz, j = k // 9, k % 9
        t3[dz * cf : (dz + 1) * cf, j * cc : (j + 1) * cc] = w3[
            k * cf : (k + 1) * cf, :
        ].astype(F32)
    turned = t3[...].T[: 9 * cc].astype(BF)
    full(a3, select(turned, 8, 0), 0, 8, near, p.x3, cc)
    v = select(jnp.broadcast_to(wh[...], (16, cf)), 10, 0)
    r = lax.broadcasted_iota(jnp.int32, (p.cells, p.cells * cf), 0)
    cell = tab[2:3, off[10] : off[11]]
    hd[...] = jnp.where(cell == r, v[0:1], 0.0).astype(BF)
    fold = lambda k: jnp.where(k < LANES, 2 * k, 2 * (k - LANES) + 1)
    r = lax.broadcasted_iota(jnp.int32, (p.span, p.span), 0)
    c = lax.broadcasted_iota(jnp.int32, (1, p.span), 1)
    pm[...] = jnp.where(r == fold(c), 1.0, 0.0).astype(BF)
    r = fold(lax.broadcasted_iota(jnp.int32, (p.span, LANES), 0))
    c = lax.broadcasted_iota(jnp.int32, (p.span, LANES), 1)
    pt[...] = jnp.where(jnp.concatenate([r - c, r - c - LANES], axis=1) == 0, 1.0, 0.0).astype(BF)
    at = 0
    for b in biases:
        n = b.shape[0]
        m = up(n, 8)
        r = lax.broadcasted_iota(jnp.int32, (m, p.nh), 0)
        v = jnp.zeros((m, p.nh), F32)
        for k in range(n):
            v = jnp.where(r == k, b[k], v)
        bias[at : at + m, :] = v
        at += m


def dot(a, b):
    return jnp.dot(a, b, preferred_element_type=F32)


def right(v):
    return pltpu.roll(v, 1, 1)


def left(v):
    return pltpu.roll(v, v.shape[1] - 1, 1)


def act(v, b):
    c = b.shape[0]
    u = v.reshape(v.shape[0] // c, c, v.shape[1]) + b[None]
    return jnp.maximum(u, 0.1 * u).reshape(v.shape).astype(BF)


def taps(e, o, n):
    even = right(o[:n]) + e[n : 2 * n] + o[2 * n :]
    odd = e[:n] + o[n : 2 * n] + left(e[2 * n :])
    return even, odd


def window(slabs, off, rows, k, cols):
    parts = [ref[base + off : base + off + rows, cols] for ref, base in slabs]
    fill = k - len(slabs) * rows
    while fill > 0:
        parts.append(parts[0][: min(fill, rows)])
        fill -= rows
    return jnp.concatenate(parts, axis=0)


def bias_rows(p, bias):
    cf, cc = p.cf, p.cc
    sizes = [cf, cf, cc, cc, cf, cf]
    at = np.concatenate([[0], np.cumsum([up(n, 8) for n in sizes])]).tolist()
    return [bias[lo : lo + n, :] for lo, n in zip(at, sizes)]


def runs(zs):
    out = []
    for z in zs:
        if out and out[-1][1] == z:
            out[-1][1] = z + 1
        else:
            out.append([z, z + 1])
    return out


def front(p, mats, blocks, dd, se, so, zs, m1, sk, po):
    a1, a2, ar, pm, b_first, b_second = mats
    cf, nh, span = p.cf, p.nh, p.span
    even_y, odd_y = slice(0, nh), slice(nh, None)
    pieces, places = [], []
    for ref, z0, x0, nx in blocks:
        nz = ref.shape[0] // nx
        for lo, hi in runs([z for z in zs if z0 <= z < z0 + nz]):
            pieces.append(ref[(lo - z0) * nx : (hi - z0) * nx, :])
            places.append((lo, hi, x0, nx))
    raw = jnp.concatenate(pieces, axis=0)
    split = [dot(raw[:, y : y + span], pm[...]) for y in range(0, p.ny, span)]
    row = 0
    for lo, hi, x0, nx in places:
        n = (hi - lo) * nx
        for k, v in enumerate(split):
            v = v[row : row + n].reshape(hi - lo, nx, span)
            for at, src in ((k * LANES, slice(0, LANES)), (nh + k * LANES, slice(LANES, None))):
                dd[lo:hi, x0 : x0 + nx, at : at + LANES] = v[:, :, src]
        row += n
    for z in zs:
        e = dd[z, :, even_y]
        o = dd[z, :, odd_y]
        pad = jnp.zeros((p.sx - 3 * p.xd, nh), F32)
        at = slice(z * p.sx, (z + 1) * p.sx)
        se[at, :] = jnp.concatenate([right(o), e, o, pad], axis=0).astype(BF)
        so[at, :] = jnp.concatenate([e, o, left(e), pad], axis=0).astype(BF)
    tail = p.k1 - 3 * p.sx
    for _, z in runs(zs):
        se[z * p.sx : z * p.sx + tail, :] = jnp.zeros((tail, nh), BF)
        so[z * p.sx : z * p.sx + tail, :] = jnp.zeros((tail, nh), BF)

    r1 = p.x1 * cf
    for z in [z for z in zs if z + 1 in zs and z + 2 in zs]:
        at = slice(z * p.sx, z * p.sx + p.k1)
        ref, to = m1[z]
        ref[to : to + r1, even_y] = act(dot(a1[...], se[at, :]), b_first)
        ref[to : to + r1, odd_y] = act(dot(a1[...], so[at, :]), b_first)

    lead = (p.x2 - p.xs) // 2

    def keep(z, s, even, odd):
        lo, hi = max(s, lead), min(s + even.shape[0] // cf, lead + p.xs)
        if lo < hi and z in sk:
            src = slice((lo - s) * cf, (hi - s) * cf)
            ref, base = sk[z]
            to = slice(base + (lo - lead) * cf, base + (hi - lead) * cf)
            ref[to, even_y] = even[src]
            ref[to, odd_y] = odd[src]

    def pairs(even, odd):
        t = even.astype(F32) + odd.astype(F32)
        t = t.reshape(t.shape[0] // (2 * cf), 2, cf, nh)
        return t[:, 0] + t[:, 1]

    def pool(zz, s, total):
        n = total.shape[0] * cf
        ref, base = po[zz]
        to = base + s // 2 * cf
        ref[to : to + n, :] = (0.125 * total).reshape(n, nh).astype(BF)

    for zz in sorted(po):
        slabs = [m1[2 * zz + k] for k in range(4)]
        for s in range(0, p.n2 * GROUP, GROUP):
            total = None
            rows = (GROUP + 2) * cf
            for dz in range(2):
                e = dot(a2[...], window(slabs[dz : dz + 3], s * cf, rows, p.k2, even_y))
                o = dot(a2[...], window(slabs[dz : dz + 3], s * cf, rows, p.k2, odd_y))
                even, odd = taps(e, o, GROUP * cf)
                even, odd = act(even, b_second), act(odd, b_second)
                keep(2 * zz + dz, s, even, odd)
                t = pairs(even, odd)
                total = t if total is None else total + t
            pool(zz, s, total)
        if p.rest:
            s = p.n2 * GROUP
            n = p.rest * cf
            rows = (p.rest + 2) * cf
            e = dot(ar[...], window(slabs, s * cf, rows, p.kr, even_y))
            o = dot(ar[...], window(slabs, s * cf, rows, p.kr, odd_y))
            even, odd = taps(e, o, 2 * n)
            even, odd = act(even, b_second), act(odd, b_second)
            keep(2 * zz, s, even[:n], odd[:n])
            keep(2 * zz + 1, s, even[n:], odd[n:])
            t = pairs(even, odd)
            pool(zz, s, t[: p.rest // 2] + t[p.rest // 2 :])


def early_kernel(plan, *refs):
    p = plan
    h = HALO
    (b0, b1, b2, a1, a2, ar, pm, bias, bh, mu, ku, pu, last, dd, se, so) = refs
    last[...] = jnp.full(last.shape, bh[0], F32)
    b_first, b_second = bias_rows(p, bias)[:2]
    xs = ((0, h), (h, p.xl), (h + p.xl, h))
    blocks = [(b, h, x, n) for b, (x, n) in zip((b0, b1, b2), xs)]
    r1, rs, rp = p.x1 * p.cf, p.xs * p.cf, p.xp * p.cf
    m1 = {h + k: (mu, k * r1) for k in range(p.zl - 2)}
    sk = {h + k: (ku, k * rs) for k in range(p.zl - 4)}
    po = {h // 2 + k: (pu, k * rp) for k in range(p.zl // 2 - 2)}
    zs = list(range(h, h + p.zl))
    front(p, (a1, a2, ar, pm, b_first, b_second), blocks, dd, se, so, zs, m1, sk, po)


def main_kernel(plan, *refs):
    p = plan
    blocks = refs[:9]
    (a1, a2, ar, a3, a4, a5, ac0, ac1, a6, hd, pm, pt, bias) = refs[9 : 9 + MATS]
    mu, ku, pu, last, out = refs[9 + MATS : 14 + MATS]
    (dd, se, so, m1, sk, po, c1, c2, de, rf) = refs[14 + MATS :]
    cf, cc, nh = p.cf, p.cc, p.nh
    h = HALO
    even_y, odd_y = slice(0, nh), slice(nh, None)
    b_first, b_second, b_third, b_fourth, b_fifth, b_sixth = bias_rows(p, bias)

    ways = lambda n: ((0, h), (h, n), (h + n, h))
    placed = [
        (blocks[3 * i + j], z, x, nx)
        for i, (z, _) in enumerate(ways(p.zl))
        for j, (x, nx) in enumerate(ways(p.xl))
    ]
    r1, rs, rp = p.x1 * cf, p.xs * cf, p.xp * cf
    lead = (p.z2 - p.zs) // 2
    done1 = range(h, h + p.zl - 2)
    done2 = range(h, h + p.zl - 4)
    donep = range(h // 2, h // 2 + p.zl // 2 - 2)
    first_at = {z: (mu, (z - h) * r1) if z in done1 else (m1, z * r1) for z in range(p.z1)}
    skip_at = {
        z: (ku, (z - h) * rs) if z in done2 else (sk, (z - lead) * rs)
        for z in range(lead, lead + p.zs)
    }
    pool_at = {
        z: (pu, (z - h // 2) * rp) if z in donep else (po, z * rp) for z in range(p.zp)
    }
    below = list(range(h + 2))
    above = list(range(h + p.zl - 2, p.zd))
    front(
        p,
        (a1, a2, ar, pm, b_first, b_second),
        placed,
        dd,
        se,
        so,
        below + above,
        first_at,
        skip_at,
        {z: v for z, v in pool_at.items() if z not in donep},
    )

    r3 = p.x3 * cc
    for z in range(p.z3):
        v = dot(a3[...], window([pool_at[z + k] for k in range(3)], 0, rp, p.k3, even_y))
        v = right(v[:r3]) + v[r3 : 2 * r3] + left(v[2 * r3 :])
        c1[z * r3 : (z + 1) * r3, :] = act(v, b_third)
    r4 = p.x4 * cc
    n4 = p.g4 * cc
    for z in range(p.z4):
        slabs = [(c1, (z + k) * r3) for k in range(3)]
        for s in p.s4:
            v = dot(a4[...], window(slabs, s * cc, n4 + 2 * cc, p.k4, even_y))
            v = right(v[:n4]) + v[n4 : 2 * n4] + left(v[2 * n4 :])
            to = z * r4 + s * cc
            c2[to : to + n4, :] = act(v, b_fourth)
    tail = p.z4 * r4
    c2[tail:, :] = jnp.zeros((c2.shape[0] - tail, nh), BF)

    r5 = p.x5 * cf
    for z in range(p.z5):
        ac = ac0 if z % 2 else ac1
        at = z // 2 * r4
        q = dot(ac[...], c2[at : at + p.kc, :])
        q0, q1, q2 = q[:r5], q[r5 : 2 * r5], q[2 * r5 :]
        slabs = [skip_at[z + lead + k] for k in range(3)]
        done = 0
        e3 = [[], [], []]
        o3 = [[], [], []]
        n = p.g5 * cf
        rows = (p.g5 + 2) * cf
        for s in p.s5:
            e = dot(a5[...], window(slabs, s * cf, rows, p.k5, even_y))
            o = dot(a5[...], window(slabs, s * cf, rows, p.k5, odd_y))
            new = (done - s) * cf
            for dy in range(3):
                e3[dy].append(e[dy * n + new : (dy + 1) * n])
                o3[dy].append(o[dy * n + new : (dy + 1) * n])
            done = s + p.g5
        e0, e1, e2 = (jnp.concatenate(v, axis=0) for v in e3)
        o0, o1, o2 = (jnp.concatenate(v, axis=0) for v in o3)
        even = right(o0 + q0) + (e1 + o2 + (q1 + q2))
        odd = (e0 + o1 + (q0 + q1)) + left(e2 + q2)
        de[z * r5 : (z + 1) * r5, even_y] = act(even, b_fifth)
        de[z * r5 : (z + 1) * r5, odd_y] = act(odd, b_fifth)
    tail = p.z5 * r5
    de[tail:, :] = jnp.zeros((de.shape[0] - tail, p.ny), BF)

    r6 = p.xl * cf
    for z in range(p.zl):
        at = slice(z * r5, z * r5 + p.k6)
        even, odd = taps(dot(a6[...], de[at, even_y]), dot(a6[...], de[at, odd_y]), r6)
        rf[z * r6 : (z + 1) * r6, even_y] = act(even, b_sixth)
        rf[z * r6 : (z + 1) * r6, odd_y] = act(odd, b_sixth)
    field = dot(hd[...], rf[...]) + last[0:1, 0:1]
    high = field.astype(BF)
    low = (field - high.astype(F32)).astype(BF)
    both = jnp.concatenate([high, low], axis=0)
    for k in range(p.ny // p.span):
        at = slice(k * LANES, (k + 1) * LANES)
        v = jnp.concatenate([both[:, at], both[:, nh + k * LANES : nh + (k + 1) * LANES]], axis=1)
        v = dot(v, pt[...])
        out[:, k * p.span : (k + 1) * p.span] = v[: p.cells] + v[p.cells :]


def shift(block, axis, step):
    count = lax.axis_size(axis)
    return lax.ppermute(block, axis, [((i + step) % count, i) for i in range(count)])


def body(
    density,
    w_first,
    b_first,
    w_second,
    b_second,
    w_third,
    b_third,
    w_fourth,
    b_fourth,
    w_fifth,
    b_fifth,
    w_sixth,
    b_sixth,
    w_head,
    b_head,
):
    zl, xl, ny = density.shape
    cf, cc = w_second.shape[0], w_third.shape[0]
    h = HALO
    p = Plan(zl, xl, ny, cf, cc)

    prev = shift(density[:, xl - h :], "tile", -1)
    after = shift(density[:, :h], "tile", 1)
    columns = [prev, density, after]
    below, above = [], []
    for c in columns:
        below.append(shift(c[zl - h :], "gz", -1))
        above.append(shift(c[:h], "gz", 1))
    below, columns, above = (
        [b.reshape(-1, ny) for b in row] for row in (below, columns, above)
    )

    def by_tap(w, *last):
        return w.transpose(2, 3, 4, *last).reshape(-1, w.shape[last[1]])

    weights = [by_tap(w, 0, 1) for w in (w_second, w_sixth, w_fifth, w_fourth)]
    weights += [by_tap(w_third, 1, 0), w_first[:, 0].transpose(1, 2, 3, 0), w_head[None]]
    biases = [b_first, b_second, b_third, b_fourth, b_fifth, b_sixth]
    tabs = p.tables()
    widths = [t.shape[1] for t in tabs]
    tab = jnp.asarray(np.concatenate(tabs, axis=1))
    bias_count = sum(up(b.shape[0], 8) for b in biases)

    mats = [
        pltpu.VMEM((p.x1 * cf, p.k1), BF),
        pltpu.VMEM((3 * GROUP * cf, p.k2), BF),
        pltpu.VMEM((max(6 * p.rest * cf, 16), p.kr), BF),
        pltpu.VMEM((3 * p.x3 * cc, p.k3), BF),
        pltpu.VMEM((3 * p.g4 * cc, p.k4), BF),
        pltpu.VMEM((3 * p.g5 * cf, p.k5), BF),
        pltpu.VMEM((3 * p.x5 * cf, p.kc), BF),
        pltpu.VMEM((3 * p.x5 * cf, p.kc), BF),
        pltpu.VMEM((3 * p.xl * cf, p.k6), BF),
        pltpu.VMEM((p.cells, p.cells * cf), BF),
        pltpu.VMEM((p.span, p.span), BF),
        pltpu.VMEM((p.span, p.span), BF),
        pltpu.VMEM((bias_count, p.nh), F32),
    ]
    vmem = pl.BlockSpec(memory_space=pltpu.VMEM)
    smem = pl.BlockSpec(memory_space=pltpu.SMEM)
    room = pltpu.CompilerParams(vmem_limit_bytes=VMEM_LIMIT)

    def in_hbm(arrays):
        return [pltpu.with_memory_space_constraint(v, pltpu.HBM) for v in arrays]

    *tables, own = pl.pallas_call(
        lambda *refs: prep_kernel(p, widths, *refs),
        in_specs=[vmem] * 8 + [smem] * 6 + [vmem],
        out_specs=[vmem] * (MATS + 1),
        out_shape=mats + [pltpu.VMEM((zl * xl, ny), BF)],
        scratch_shapes=[pltpu.VMEM((72, LANES), F32), pltpu.VMEM((LANES, up(9 * cc, LANES)), F32)],
        name="bands",
    )(*in_hbm([tab] + weights), *biases, *in_hbm([columns[1]]))
    columns[1] = own

    def on_chip(arrays):
        return [pltpu.with_memory_space_constraint(v, pltpu.VMEM) for v in arrays]

    stacks = [
        pltpu.VMEM((p.zd, p.xd, ny), F32),
        pltpu.VMEM((p.zd * p.sx + 256, p.nh), BF),
        pltpu.VMEM((p.zd * p.sx + 256, p.nh), BF),
    ]
    ready = pl.pallas_call(
        lambda *refs: early_kernel(p, *refs),
        in_specs=[vmem] * 8 + [smem],
        out_specs=[vmem] * 4,
        out_shape=[
            pltpu.VMEM(((zl - 2) * p.x1 * cf, ny), BF),
            pltpu.VMEM(((zl - 4) * p.xs * cf, ny), BF),
            pltpu.VMEM(((zl // 2 - 2) * p.xp * cf, p.nh), BF),
            pltpu.VMEM((8, LANES), F32),
        ],
        scratch_shapes=stacks,
        compiler_params=room,
        name="early",
    )(*on_chip(columns), *on_chip([tables[k] for k in (0, 1, 2, 10, 12)]), b_head)

    field = pl.pallas_call(
        lambda *refs: main_kernel(p, *refs),
        in_specs=[vmem] * (9 + MATS + 4),
        out_specs=vmem,
        out_shape=jax.ShapeDtypeStruct((p.cells, ny), F32),
        scratch_shapes=stacks
        + [
            pltpu.VMEM((p.z1 * p.x1 * cf, ny), BF),
            pltpu.VMEM((p.zs * p.xs * cf, ny), BF),
            pltpu.VMEM((p.zp * p.xp * cf, p.nh), BF),
            pltpu.VMEM((p.z3 * p.x3 * cc, p.nh), BF),
            pltpu.VMEM((p.z4 * p.x4 * cc + 256, p.nh), BF),
            pltpu.VMEM((p.z5 * p.x5 * cf + 256, ny), BF),
            pltpu.VMEM((p.cells * cf, ny), BF),
        ],
        compiler_params=room,
        name="unet",
    )(*on_chip(below + columns + above), *on_chip(tables), *on_chip(ready))
    return field.reshape(zl, xl, ny)


def solution(mesh):
    return jax.shard_map(
        body,
        mesh=mesh,
        in_specs=(P("gz", "tile", None),) + (P(),) * 14,
        out_specs=P("gz", "tile", None),
        check_vma=False,
    )
```

time: 25.6 us -> 25.5 us (level); the launches traced: 25.1 us -> 25.3 us
    pallas_call x0 -> x1, Pallas kernels: none -> 1.35 us  [body(): pl.pallas_call(lambda *refs: early_kernel(p, *refs), in_specs=[vmem] * 8...]
    pallas_call x1, Pallas kernels: 7.96 us -> 7.11 us  [body(): pl.pallas_call(lambda *refs: main_kernel(p, *refs), in_specs=[vmem] * (9...]
    pallas_call x1, Pallas kernels: 2.11 us -> 1.84 us  [body(): pl.pallas_call(lambda *refs: prep_kernel(p, widths, *refs), in_specs=[vme...]
  transfers between devices with their start and end apart: 8 -> 8, of which waited for: 1 -> 1; matrix products, arithmetic and copies ran while one was open for 0% -> 0% of each run, Pallas kernels for 8% -> 13%
where the time goes in v3:
time: 25.5 us; the launch traced here: 25.3 us
  starting transfers between devices  12.6 us (49%)
  Pallas kernels  10.3 us (40%)
  waiting for transfers between devices  1.74 us (7%)
  between operations  0.71 us (3%)
    ppermute x8, starting transfers between devices, shift(): lax.ppermute(block, axis, [((i + step) % count, i) for i in range(count)])  12.6 us
    pallas_call x1, Pallas kernels, body(): pl.pallas_call(lambda *refs: main_kernel(p, *refs), in_specs=[vmem] * (9...  7.11 us
    pallas_call x1, Pallas kernels, body(): pl.pallas_call(lambda *refs: prep_kernel(p, widths, *refs), in_specs=[vme...  1.84 us
    ppermute x8, waiting for transfers between devices, shift(): lax.ppermute(block, axis, [((i + step) % count, i) for i in range(count)])  1.74 us
    pallas_call x1, Pallas kernels, body(): pl.pallas_call(lambda *refs: early_kernel(p, *refs), in_specs=[vmem] * 8...  1.35 us
  transfers between devices with their start and end apart: 8, of which 1 were waited for; matrix products, arithmetic and copies ran while one was open for 0% of the time, Pallas kernels for 13%

profile of v3, /device:TPU:1, one launch (start us, length us, event | category | flops | bytes accessed | tf_op | source)
XLA Modules:
  0.0 25.3 jit_solution(6886556740429859949)
XLA Ops:
  0.0 5.1 %collective-permute-start.3 = (bf16[8,8,512]{2,1,0:T(8,128)(2,1)}, bf16[8,8,512]{2,1,0:T(8,128)(2,1)S(1)}, u32[]{:S(2)}, u32[]{:S(2)}) collective-permute-start(bf16[8,8,512]{2,1,0:T(8,128)(2,1)} %param.16), channel_id=1, source_target_pairs={{1,0},{2,1},{3,2},{4,3},{5,4},{6,5},{7,6},{0,7},{9,8},{10,9},{11,1... | collective-permute-start | bytes 196616 | tf_op jit(solution)/shard_map/ppermute | solution.py:487
  5.1 0.0 collective-permute-start
  5.1 2.1 %collective-permute-start.2 = (bf16[8,8,512]{2,1,0:T(8,128)(2,1)}, bf16[8,8,512]{2,1,0:T(8,128)(2,1)S(1)}, u32[]{:S(2)}, u32[]{:S(2)}) collective-permute-start(bf16[8,8,512]{2,1,0:T(8,128)(2,1)} %param.16), channel_id=1, source_target_pairs={{24,0},{0,8},{8,16},{16,24},{25,1},{1,9},{9,17},{17,25},{26,2},{2,... | collective-permute-start | bytes 196616 | tf_op jit(solution)/shard_map/ppermute | solution.py:487
  7.2 0.0 collective-permute-start.6
  7.2 0.0 collective-permute-done.3
  7.2 1.1 %collective-permute-start.7 = (bf16[8,8,512]{2,1,0:T(8,128)(2,1)S(1)}, bf16[8,8,512]{2,1,0:T(8,128)(2,1)S(1)}, u32[]{:S(2)}, u32[]{:S(2)}) collective-permute-start(bf16[8,8,512]{2,1,0:T(8,128)(2,1)S(1)} %collective-permute-done.3), channel_id=1, source_target_pairs={{8,0},{16,8},{24,16},{0,24},{9,1},{17,9},{25,17},{1,25},{10,2},{18... | collective-permute-start | bytes 196616 | tf_op jit(solution)/shard_map/ppermute | solution.py:487
  8.2 1.1 %collective-permute-start.4 = (bf16[8,8,512]{2,1,0:T(8,128)(2,1)S(1)}, bf16[8,8,512]{2,1,0:T(8,128)(2,1)S(1)}, u32[]{:S(2)}, u32[]{:S(2)}) collective-permute-start(bf16[8,8,512]{2,1,0:T(8,128)(2,1)S(1)} %collective-permute-done.3), channel_id=1, source_target_pairs={{24,0},{0,8},{8,16},{16,24},{25,1},{1,9},{9,17},{17,25},{26,2},{2,... | collective-permute-start | bytes 196616 | tf_op jit(solution)/shard_map/ppermute | solution.py:487
  9.4 1.7 %collective-permute-done = bf16[8,8,512]{2,1,0:T(8,128)(2,1)S(1)} collective-permute-done((bf16[8,8,512]{2,1,0:T(8,128)(2,1)}, bf16[8,8,512]{2,1,0:T(8,128)(2,1)S(1)}, u32[]{:S(2)}, u32[]{:S(2)}) %collective-permute-start) | collective-permute-done | bytes 65568 | tf_op jit(solution)/shard_map/ppermute | solution.py:487
  11.1 2.1 %collective-permute-start.5 = (bf16[8,8,512]{2,1,0:T(8,128)(2,1)S(1)}, bf16[8,8,512]{2,1,0:T(8,128)(2,1)S(1)}, u32[]{:S(2)}, u32[]{:S(2)}) collective-permute-start(bf16[8,8,512]{2,1,0:T(8,128)(2,1)S(1)} %collective-permute-done), channel_id=1, source_target_pairs={{8,0},{16,8},{24,16},{0,24},{9,1},{17,9},{25,17},{1,25},{10,2},{18... | collective-permute-start | bytes 196616 | tf_op jit(solution)/shard_map/ppermute | solution.py:487
  13.2 0.0 collective-permute-done.2
  13.2 1.1 %collective-permute-start.1 = (bf16[8,8,512]{2,1,0:T(8,128)(2,1)S(1)}, bf16[8,8,512]{2,1,0:T(8,128)(2,1)S(1)}, u32[]{:S(2)}, u32[]{:S(2)}) collective-permute-start(bf16[8,8,512]{2,1,0:T(8,128)(2,1)S(1)} %collective-permute-done), channel_id=1, source_target_pairs={{24,0},{0,8},{8,16},{16,24},{25,1},{1,9},{9,17},{17,25},{26,2},{2,... | collective-permute-start | bytes 196616 | tf_op jit(solution)/shard_map/ppermute | solution.py:487
  15.0 1.8 %bands.1 = (bf16[176,256]{1,0:T(8,128)(2,1)S(1)}, bf16[192,256]{1,0:T(8,128)(2,1)S(1)}, bf16[192,256]{1,0:T(8,128)(2,1)S(1)}, bf16[384,256]{1,0:T(8,128)(2,1)S(1...) custom-call(s32[3,3072]{1,0:T(4,128)} %constant.2.clone.refs_0_, ...), custom_call_target="tpu_custom_call" | custom-call | tf_op jit(solution)/shard_map/bands/pallas_call | solution.py:556
  16.8 1.4 %early.1 = (bf16[1056,512]{1,0:T(8,128)(2,1)S(1)}, bf16[384,512]{1,0:T(8,128)(2,1)S(1)}, bf16[160,256]{1,0:T(8,128)(2,1)S(1)}, f32[8,128]{1,0:T(8,128)S(1)}) custom-call(bf16[64,512]{1,0:T(8,128)(2,1)S(1)} %bitcast.31, bf16[64,512]{1,0:T(8,128)(2,1)S(1)} %get-tuple-element.23.refs_1_.refs_4_, bf16[64,512]{1,0:T(8,128)(2,1)S(1)} %bitcast.29, ...), custom_call_target="tpu_custom_call" | custom-call | tf_op jit(solution)/shard_map/early/pallas_call | solution.py:574
  18.2 0.0 collective-permute-done.6
  18.2 0.0 collective-permute-done.7
  18.2 0.0 collective-permute-done.4
  18.2 0.0 collective-permute-done.5
  18.2 0.0 collective-permute-done.1
  18.2 7.1 %unet.1 = f32[64,512]{1,0:T(8,128)} custom-call(bf16[64,512]{1,0:T(8,128)(2,1)S(1)} %bitcast.38, bf16[64,512]{1,0:T(8,128)(2,1)S(1)} %bitcast.33, bf16[64,512]{1,0:T(8,128)(2,1)S(1)} %bitcast.36, bf16[64,512]{1,0:T(8,128)(2,1)S(1)} %bitcast.32, bf16[64,512]{1,0:T(8,128)(2,1)S(1)} %get-tuple-element.23.refs_1_.refs_4_, bf16[64,512]{1,0:T(8,128)(2,1)S(1)} %bitcast.30, ...), custom_call_target="tpu_custom_call" | custom-call | tf_op jit(solution)/shard_map/unet/pallas_call | solution.py:589
Async XLA Ops:
  0.0 7.2 %collective-permute-start.3 = (bf16[8,8,512]{2,1,0:T(8,128)(2,1)}, bf16[8,8,512]{2,1,0:T(8,128)(2,1)S(1)}, u32[]{:S(2)}, u32[]{:S(2)}) collective-permute-start(bf16[8,8,512]{2,1,0:T(8,128)(2,1)} %param.16), channel_id=1, source_target_pairs={{1,0},{2,1},{3,2},{4,3},{5,4},{6,5},{7,6},{0,7},{9,8},{10,9},{11,1... | collective-permute-start | bytes 196616 | tf_op jit(solution)/shard_map/ppermute | solution.py:487
  5.1 6.0 %collective-permute-start = (bf16[8,8,512]{2,1,0:T(8,128)(2,1)}, bf16[8,8,512]{2,1,0:T(8,128)(2,1)S(1)}, u32[]{:S(2)}, u32[]{:S(2)}) collective-permute-start(bf16[8,8,512]{2,1,0:T(8,128)(2,1)} %param.16), channel_id=1, source_target_pairs={{7,0},{0,1},{1,2},{2,3},{3,4},{4,5},{5,6},{6,7},{15,8},{8,9},{9,10... | collective-permute-start | bytes 196616 | tf_op jit(solution)/shard_map/ppermute | solution.py:487
  5.1 8.1 %collective-permute-start.2 = (bf16[8,8,512]{2,1,0:T(8,128)(2,1)}, bf16[8,8,512]{2,1,0:T(8,128)(2,1)S(1)}, u32[]{:S(2)}, u32[]{:S(2)}) collective-permute-start(bf16[8,8,512]{2,1,0:T(8,128)(2,1)} %param.16), channel_id=1, source_target_pairs={{24,0},{0,8},{8,16},{16,24},{25,1},{1,9},{9,17},{17,25},{26,2},{2,... | collective-permute-start | bytes 196616 | tf_op jit(solution)/shard_map/ppermute | solution.py:487
  7.2 11.0 %collective-permute-start.6 = (bf16[8,8,512]{2,1,0:T(8,128)(2,1)}, bf16[8,8,512]{2,1,0:T(8,128)(2,1)S(1)}, u32[]{:S(2)}, u32[]{:S(2)}) collective-permute-start(bf16[8,8,512]{2,1,0:T(8,128)(2,1)} %param.16), channel_id=1, source_target_pairs={{8,0},{16,8},{24,16},{0,24},{9,1},{17,9},{25,17},{1,25},{10,2},{18... | collective-permute-start | bytes 196616 | tf_op jit(solution)/shard_map/ppermute | solution.py:487
  7.2 11.0 %collective-permute-start.7 = (bf16[8,8,512]{2,1,0:T(8,128)(2,1)S(1)}, bf16[8,8,512]{2,1,0:T(8,128)(2,1)S(1)}, u32[]{:S(2)}, u32[]{:S(2)}) collective-permute-start(bf16[8,8,512]{2,1,0:T(8,128)(2,1)S(1)} %collective-permute-done.3), channel_id=1, source_target_pairs={{8,0},{16,8},{24,16},{0,24},{9,1},{17,9},{25,17},{1,25},{10,2},{18... | collective-permute-start | bytes 196616 | tf_op jit(solution)/shard_map/ppermute | solution.py:487
  8.2 10.0 %collective-permute-start.4 = (bf16[8,8,512]{2,1,0:T(8,128)(2,1)S(1)}, bf16[8,8,512]{2,1,0:T(8,128)(2,1)S(1)}, u32[]{:S(2)}, u32[]{:S(2)}) collective-permute-start(bf16[8,8,512]{2,1,0:T(8,128)(2,1)S(1)} %collective-permute-done.3), channel_id=1, source_target_pairs={{24,0},{0,8},{8,16},{16,24},{25,1},{1,9},{9,17},{17,25},{26,2},{2,... | collective-permute-start | bytes 196616 | tf_op jit(solution)/shard_map/ppermute | solution.py:487
  11.1 7.1 %collective-permute-start.5 = (bf16[8,8,512]{2,1,0:T(8,128)(2,1)S(1)}, bf16[8,8,512]{2,1,0:T(8,128)(2,1)S(1)}, u32[]{:S(2)}, u32[]{:S(2)}) collective-permute-start(bf16[8,8,512]{2,1,0:T(8,128)(2,1)S(1)} %collective-permute-done), channel_id=1, source_target_pairs={{8,0},{16,8},{24,16},{0,24},{9,1},{17,9},{25,17},{1,25},{10,2},{18... | collective-permute-start | bytes 196616 | tf_op jit(solution)/shard_map/ppermute | solution.py:487
  13.2 5.0 %collective-permute-start.1 = (bf16[8,8,512]{2,1,0:T(8,128)(2,1)S(1)}, bf16[8,8,512]{2,1,0:T(8,128)(2,1)S(1)}, u32[]{:S(2)}, u32[]{:S(2)}) collective-permute-start(bf16[8,8,512]{2,1,0:T(8,128)(2,1)S(1)} %collective-permute-done), channel_id=1, source_target_pairs={{24,0},{0,8},{8,16},{16,24},{25,1},{1,9},{9,17},{17,25},{26,2},{2,... | collective-permute-start | bytes 196616 | tf_op jit(solution)/shard_map/ppermute | solution.py:487

commit v4 on v3

--- a/solution.py
+++ b/solution.py
@@ -273,29 +273,30 @@
     a1, a2, ar, pm, b_first, b_second = mats
     cf, nh, span = p.cf, p.nh, p.span
     even_y, odd_y = slice(0, nh), slice(nh, None)
-    pieces, places = [], []
-    for ref, z0, x0, nx in blocks:
-        nz = ref.shape[0] // nx
-        for lo, hi in runs([z for z in zs if z0 <= z < z0 + nz]):
-            pieces.append(ref[(lo - z0) * nx : (hi - z0) * nx, :])
-            places.append((lo, hi, x0, nx))
-    raw = jnp.concatenate(pieces, axis=0)
-    split = [dot(raw[:, y : y + span], pm[...]) for y in range(0, p.ny, span)]
-    row = 0
-    for lo, hi, x0, nx in places:
-        n = (hi - lo) * nx
-        for k, v in enumerate(split):
-            v = v[row : row + n].reshape(hi - lo, nx, span)
-            for at, src in ((k * LANES, slice(0, LANES)), (nh + k * LANES, slice(LANES, None))):
-                dd[lo:hi, x0 : x0 + nx, at : at + LANES] = v[:, :, src]
-        row += n
-    for z in zs:
-        e = dd[z, :, even_y]
-        o = dd[z, :, odd_y]
-        pad = jnp.zeros((p.sx - 3 * p.xd, nh), F32)
-        at = slice(z * p.sx, (z + 1) * p.sx)
-        se[at, :] = jnp.concatenate([right(o), e, o, pad], axis=0).astype(BF)
-        so[at, :] = jnp.concatenate([e, o, left(e), pad], axis=0).astype(BF)
+    for first_z, end_z in runs(zs):
+        pieces, places = [], []
+        for ref, z0, x0, nx in blocks:
+            lo, hi = max(z0, first_z), min(z0 + ref.shape[0] // nx, end_z)
+            if lo < hi:
+                pieces.append(ref[(lo - z0) * nx : (hi - z0) * nx, :])
+                places.append((lo, hi, x0, nx))
+        raw = jnp.concatenate(pieces, axis=0)
+        split = [dot(raw[:, y : y + span], pm[...]) for y in range(0, p.ny, span)]
+        row = 0
+        for lo, hi, x0, nx in places:
+            n = (hi - lo) * nx
+            for k, v in enumerate(split):
+                v = v[row : row + n].reshape(hi - lo, nx, span)
+                for at, src in ((k * LANES, slice(0, LANES)), (nh + k * LANES, slice(LANES, None))):
+                    dd[lo:hi, x0 : x0 + nx, at : at + LANES] = v[:, :, src]
+            row += n
+        for z in range(first_z, end_z):
+            e = dd[z, :, even_y]
+            o = dd[z, :, odd_y]
+            pad = jnp.zeros((p.sx - 3 * p.xd, nh), F32)
+            at = slice(z * p.sx, (z + 1) * p.sx)
+            se[at, :] = jnp.concatenate([right(o), e, o, pad], axis=0).astype(BF)
+            so[at, :] = jnp.concatenate([e, o, left(e), pad], axis=0).astype(BF)
     tail = p.k1 - 3 * p.sx
     for _, z in runs(zs):
         se[z * p.sx : z * p.sx + tail, :] = jnp.zeros((tail, nh), BF)
@@ -358,11 +359,14 @@
             pool(zz, s, t[: p.rest // 2] + t[p.rest // 2 :])
 
 
+def offset_kernel(value, out):
+    out[...] = jnp.full(out.shape, value[0], F32)
+
+
 def early_kernel(plan, *refs):
     p = plan
     h = HALO
-    (b0, b1, b2, a1, a2, ar, pm, bias, bh, mu, ku, pu, last, dd, se, so) = refs
-    last[...] = jnp.full(last.shape, bh[0], F32)
+    (b0, b1, b2, a1, a2, ar, pm, bias, mu, ku, pu, dd, se, so) = refs
     b_first, b_second = bias_rows(p, bias)[:2]
     xs = ((0, h), (h, p.xl), (h + p.xl, h))
     blocks = [(b, h, x, n) for b, (x, n) in zip((b0, b1, b2), xs)]
@@ -566,6 +570,14 @@
     def on_chip(arrays):
         return [pltpu.with_memory_space_constraint(v, pltpu.VMEM) for v in arrays]
 
+    last = pl.pallas_call(
+        offset_kernel,
+        in_specs=[smem],
+        out_specs=vmem,
+        out_shape=pltpu.VMEM((8, LANES), F32),
+        name="offset",
+    )(b_head)
+
     stacks = [
         pltpu.VMEM((p.zd, p.xd, ny), F32),
         pltpu.VMEM((p.zd * p.sx + 256, p.nh), BF),
@@ -573,18 +585,17 @@
     ]
     ready = pl.pallas_call(
         lambda *refs: early_kernel(p, *refs),
-        in_specs=[vmem] * 8 + [smem],
-        out_specs=[vmem] * 4,
+        in_specs=[vmem] * 8,
+        out_specs=[vmem] * 3,
         out_shape=[
             pltpu.VMEM(((zl - 2) * p.x1 * cf, ny), BF),
             pltpu.VMEM(((zl - 4) * p.xs * cf, ny), BF),
             pltpu.VMEM(((zl // 2 - 2) * p.xp * cf, p.nh), BF),
-            pltpu.VMEM((8, LANES), F32),
         ],
         scratch_shapes=stacks,
         compiler_params=room,
         name="early",
-    )(*on_chip(columns), *on_chip([tables[k] for k in (0, 1, 2, 10, 12)]), b_head)
+    )(*on_chip(columns), *on_chip([tables[k] for k in (0, 1, 2, 10, 12)]))
 
     field = pl.pallas_call(
         lambda *refs: main_kernel(p, *refs),
@@ -603,7 +614,7 @@
         ],
         compiler_params=room,
         name="unet",
-    )(*on_chip(below + columns + above), *on_chip(tables), *on_chip(ready))
+    )(*on_chip(below + columns + above), *on_chip(tables), *on_chip(list(ready) + [last]))
     return field.reshape(zl, xl, ny)
 
 

time: 25.5 us -> 25.5 us (level)
    pallas_call x1 -> x2, Pallas kernels: 1.35 us -> 1.36 us  [the longest x1 1.35 us: body(): pl.pallas_call(lambda *refs: early_kernel(p, *refs), in_specs=[vmem] * 8,...]
where the time goes in v4:
time: 25.5 us; the launch traced here: 25.4 us
  starting transfers between devices  12.6 us (49%)
  Pallas kernels  10.3 us (40%)
  waiting for transfers between devices  1.74 us (7%)
  between operations  0.72 us (3%)
    ppermute x8, starting transfers between devices, shift(): lax.ppermute(block, axis, [((i + step) % count, i) for i in range(count)])  12.6 us
    pallas_call x1, Pallas kernels, body(): pl.pallas_call(lambda *refs: main_kernel(p, *refs), in_specs=[vmem] * (9...  7.12 us
    pallas_call x1, Pallas kernels, body(): pl.pallas_call(lambda *refs: prep_kernel(p, widths, *refs), in_specs=[vme...  1.84 us
    ppermute x8, waiting for transfers between devices, shift(): lax.ppermute(block, axis, [((i + step) % count, i) for i in range(count)])  1.74 us
    pallas_call x1, Pallas kernels, body(): pl.pallas_call(lambda *refs: early_kernel(p, *refs), in_specs=[vmem] * 8,...  1.35 us
  transfers between devices with their start and end apart: 8, of which 1 were waited for; matrix products, arithmetic and copies ran while one was open for 0% of the time, Pallas kernels for 13%

profile of v4, /device:TPU:1, one launch (start us, length us, event | category | flops | bytes accessed | tf_op | source)
XLA Modules:
  0.0 25.4 jit_solution(12605438364279460059)
XLA Ops:
  0.0 5.1 %collective-permute-start.3 = (bf16[8,8,512]{2,1,0:T(8,128)(2,1)}, bf16[8,8,512]{2,1,0:T(8,128)(2,1)S(1)}, u32[]{:S(2)}, u32[]{:S(2)}) collective-permute-start(bf16[8,8,512]{2,1,0:T(8,128)(2,1)} %param.16), channel_id=1, source_target_pairs={{1,0},{2,1},{3,2},{4,3},{5,4},{6,5},{7,6},{0,7},{9,8},{10,9},{11,1... | collective-permute-start | bytes 196616 | tf_op jit(solution)/shard_map/ppermute | solution.py:491
  5.1 0.0 collective-permute-start
  5.1 2.1 %collective-permute-start.2 = (bf16[8,8,512]{2,1,0:T(8,128)(2,1)}, bf16[8,8,512]{2,1,0:T(8,128)(2,1)S(1)}, u32[]{:S(2)}, u32[]{:S(2)}) collective-permute-start(bf16[8,8,512]{2,1,0:T(8,128)(2,1)} %param.16), channel_id=1, source_target_pairs={{24,0},{0,8},{8,16},{16,24},{25,1},{1,9},{9,17},{17,25},{26,2},{2,... | collective-permute-start | bytes 196616 | tf_op jit(solution)/shard_map/ppermute | solution.py:491
  7.2 0.0 collective-permute-start.6
  7.2 0.0 collective-permute-done.3
  7.2 1.1 %collective-permute-start.7 = (bf16[8,8,512]{2,1,0:T(8,128)(2,1)S(1)}, bf16[8,8,512]{2,1,0:T(8,128)(2,1)S(1)}, u32[]{:S(2)}, u32[]{:S(2)}) collective-permute-start(bf16[8,8,512]{2,1,0:T(8,128)(2,1)S(1)} %collective-permute-done.3), channel_id=1, source_target_pairs={{8,0},{16,8},{24,16},{0,24},{9,1},{17,9},{25,17},{1,25},{10,2},{18... | collective-permute-start | bytes 196616 | tf_op jit(solution)/shard_map/ppermute | solution.py:491
  8.2 1.1 %collective-permute-start.4 = (bf16[8,8,512]{2,1,0:T(8,128)(2,1)S(1)}, bf16[8,8,512]{2,1,0:T(8,128)(2,1)S(1)}, u32[]{:S(2)}, u32[]{:S(2)}) collective-permute-start(bf16[8,8,512]{2,1,0:T(8,128)(2,1)S(1)} %collective-permute-done.3), channel_id=1, source_target_pairs={{24,0},{0,8},{8,16},{16,24},{25,1},{1,9},{9,17},{17,25},{26,2},{2,... | collective-permute-start | bytes 196616 | tf_op jit(solution)/shard_map/ppermute | solution.py:491
  9.4 1.7 %collective-permute-done = bf16[8,8,512]{2,1,0:T(8,128)(2,1)S(1)} collective-permute-done((bf16[8,8,512]{2,1,0:T(8,128)(2,1)}, bf16[8,8,512]{2,1,0:T(8,128)(2,1)S(1)}, u32[]{:S(2)}, u32[]{:S(2)}) %collective-permute-start) | collective-permute-done | bytes 65568 | tf_op jit(solution)/shard_map/ppermute | solution.py:491
  11.1 2.1 %collective-permute-start.5 = (bf16[8,8,512]{2,1,0:T(8,128)(2,1)S(1)}, bf16[8,8,512]{2,1,0:T(8,128)(2,1)S(1)}, u32[]{:S(2)}, u32[]{:S(2)}) collective-permute-start(bf16[8,8,512]{2,1,0:T(8,128)(2,1)S(1)} %collective-permute-done), channel_id=1, source_target_pairs={{8,0},{16,8},{24,16},{0,24},{9,1},{17,9},{25,17},{1,25},{10,2},{18... | collective-permute-start | bytes 196616 | tf_op jit(solution)/shard_map/ppermute | solution.py:491
  13.2 0.0 collective-permute-done.2
  13.2 1.1 %collective-permute-start.1 = (bf16[8,8,512]{2,1,0:T(8,128)(2,1)S(1)}, bf16[8,8,512]{2,1,0:T(8,128)(2,1)S(1)}, u32[]{:S(2)}, u32[]{:S(2)}) collective-permute-start(bf16[8,8,512]{2,1,0:T(8,128)(2,1)S(1)} %collective-permute-done), channel_id=1, source_target_pairs={{24,0},{0,8},{8,16},{16,24},{25,1},{1,9},{9,17},{17,25},{26,2},{2,... | collective-permute-start | bytes 196616 | tf_op jit(solution)/shard_map/ppermute | solution.py:491
  15.0 1.8 %bands.1 = (bf16[176,256]{1,0:T(8,128)(2,1)S(1)}, bf16[192,256]{1,0:T(8,128)(2,1)S(1)}, bf16[192,256]{1,0:T(8,128)(2,1)S(1)}, bf16[384,256]{1,0:T(8,128)(2,1)S(1...) custom-call(s32[3,3072]{1,0:T(4,128)} %constant.2.clone.refs_0_, ...), custom_call_target="tpu_custom_call" | custom-call | tf_op jit(solution)/shard_map/bands/pallas_call | solution.py:560
  16.8 1.4 %early.1 = (bf16[1056,512]{1,0:T(8,128)(2,1)S(1)}, bf16[384,512]{1,0:T(8,128)(2,1)S(1)}, bf16[160,256]{1,0:T(8,128)(2,1)S(1)}) custom-call(bf16[64,512]{1,0:T(8,128)(2,1)S(1)} %bitcast.31, bf16[64,512]{1,0:T(8,128)(2,1)S(1)} %get-tuple-element.22.refs_1_.refs_4_, bf16[64,512]{1,0:T(8,128)(2,1)S(1)} %bitcast.29, ...), custom_call_target="tpu_custom_call" | custom-call | tf_op jit(solution)/shard_map/early/pallas_call | solution.py:586
  18.2 0.0 collective-permute-done.6
  18.2 0.0 collective-permute-done.7
  18.2 0.0 collective-permute-done.4
  18.2 0.0 collective-permute-done.5
  18.2 0.0 collective-permute-done.1
  18.3 7.1 %unet.1 = f32[64,512]{1,0:T(8,128)} custom-call(bf16[64,512]{1,0:T(8,128)(2,1)S(1)} %bitcast.38, bf16[64,512]{1,0:T(8,128)(2,1)S(1)} %bitcast.33, bf16[64,512]{1,0:T(8,128)(2,1)S(1)} %bitcast.36, bf16[64,512]{1,0:T(8,128)(2,1)S(1)} %bitcast.32, bf16[64,512]{1,0:T(8,128)(2,1)S(1)} %get-tuple-element.22.refs_1_.refs_4_, bf16[64,512]{1,0:T(8,128)(2,1)S(1)} %bitcast.30, ...), custom_call_target="tpu_custom_call" | custom-call | tf_op jit(solution)/shard_map/unet/pallas_call | solution.py:600
  (1 shorter events, 0.0 us)
Async XLA Ops:
  0.0 7.2 %collective-permute-start.3 = (bf16[8,8,512]{2,1,0:T(8,128)(2,1)}, bf16[8,8,512]{2,1,0:T(8,128)(2,1)S(1)}, u32[]{:S(2)}, u32[]{:S(2)}) collective-permute-start(bf16[8,8,512]{2,1,0:T(8,128)(2,1)} %param.16), channel_id=1, source_target_pairs={{1,0},{2,1},{3,2},{4,3},{5,4},{6,5},{7,6},{0,7},{9,8},{10,9},{11,1... | collective-permute-start | bytes 196616 | tf_op jit(solution)/shard_map/ppermute | solution.py:491
  5.1 6.0 %collective-permute-start = (bf16[8,8,512]{2,1,0:T(8,128)(2,1)}, bf16[8,8,512]{2,1,0:T(8,128)(2,1)S(1)}, u32[]{:S(2)}, u32[]{:S(2)}) collective-permute-start(bf16[8,8,512]{2,1,0:T(8,128)(2,1)} %param.16), channel_id=1, source_target_pairs={{7,0},{0,1},{1,2},{2,3},{3,4},{4,5},{5,6},{6,7},{15,8},{8,9},{9,10... | collective-permute-start | bytes 196616 | tf_op jit(solution)/shard_map/ppermute | solution.py:491
  5.1 8.1 %collective-permute-start.2 = (bf16[8,8,512]{2,1,0:T(8,128)(2,1)}, bf16[8,8,512]{2,1,0:T(8,128)(2,1)S(1)}, u32[]{:S(2)}, u32[]{:S(2)}) collective-permute-start(bf16[8,8,512]{2,1,0:T(8,128)(2,1)} %param.16), channel_id=1, source_target_pairs={{24,0},{0,8},{8,16},{16,24},{25,1},{1,9},{9,17},{17,25},{26,2},{2,... | collective-permute-start | bytes 196616 | tf_op jit(solution)/shard_map/ppermute | solution.py:491
  7.2 11.0 %collective-permute-start.6 = (bf16[8,8,512]{2,1,0:T(8,128)(2,1)}, bf16[8,8,512]{2,1,0:T(8,128)(2,1)S(1)}, u32[]{:S(2)}, u32[]{:S(2)}) collective-permute-start(bf16[8,8,512]{2,1,0:T(8,128)(2,1)} %param.16), channel_id=1, source_target_pairs={{8,0},{16,8},{24,16},{0,24},{9,1},{17,9},{25,17},{1,25},{10,2},{18... | collective-permute-start | bytes 196616 | tf_op jit(solution)/shard_map/ppermute | solution.py:491
  7.2 11.1 %collective-permute-start.7 = (bf16[8,8,512]{2,1,0:T(8,128)(2,1)S(1)}, bf16[8,8,512]{2,1,0:T(8,128)(2,1)S(1)}, u32[]{:S(2)}, u32[]{:S(2)}) collective-permute-start(bf16[8,8,512]{2,1,0:T(8,128)(2,1)S(1)} %collective-permute-done.3), channel_id=1, source_target_pairs={{8,0},{16,8},{24,16},{0,24},{9,1},{17,9},{25,17},{1,25},{10,2},{18... | collective-permute-start | bytes 196616 | tf_op jit(solution)/shard_map/ppermute | solution.py:491
  8.2 10.0 %collective-permute-start.4 = (bf16[8,8,512]{2,1,0:T(8,128)(2,1)S(1)}, bf16[8,8,512]{2,1,0:T(8,128)(2,1)S(1)}, u32[]{:S(2)}, u32[]{:S(2)}) collective-permute-start(bf16[8,8,512]{2,1,0:T(8,128)(2,1)S(1)} %collective-permute-done.3), channel_id=1, source_target_pairs={{24,0},{0,8},{8,16},{16,24},{25,1},{1,9},{9,17},{17,25},{26,2},{2,... | collective-permute-start | bytes 196616 | tf_op jit(solution)/shard_map/ppermute | solution.py:491
  11.1 7.1 %collective-permute-start.5 = (bf16[8,8,512]{2,1,0:T(8,128)(2,1)S(1)}, bf16[8,8,512]{2,1,0:T(8,128)(2,1)S(1)}, u32[]{:S(2)}, u32[]{:S(2)}) collective-permute-start(bf16[8,8,512]{2,1,0:T(8,128)(2,1)S(1)} %collective-permute-done), channel_id=1, source_target_pairs={{8,0},{16,8},{24,16},{0,24},{9,1},{17,9},{25,17},{1,25},{10,2},{18... | collective-permute-start | bytes 196616 | tf_op jit(solution)/shard_map/ppermute | solution.py:491
  13.2 5.0 %collective-permute-start.1 = (bf16[8,8,512]{2,1,0:T(8,128)(2,1)S(1)}, bf16[8,8,512]{2,1,0:T(8,128)(2,1)S(1)}, u32[]{:S(2)}, u32[]{:S(2)}) collective-permute-start(bf16[8,8,512]{2,1,0:T(8,128)(2,1)S(1)} %collective-permute-done), channel_id=1, source_target_pairs={{24,0},{0,8},{8,16},{16,24},{25,1},{1,9},{9,17},{17,25},{26,2},{2,... | collective-permute-start | bytes 196616 | tf_op jit(solution)/shard_map/ppermute | solution.py:491
